TPU v7x, 256 devices: a whole 4x4x8 slice. The times are simulated.
256 devices in a mesh: gx: 8 (over x, core), gy: 32 (over y, z).
Axes of the slice: x: 4, y: 4, z: 8, core: 2. Of those that a mesh axis runs over, the one named last changes fastest.
Arguments:
- features: bfloat16 [65536, 128], P(('gx', 'gy')), may hold values from -6 to 6
- tile_vals: bfloat16 [16384, 128, 128], P(('gx', 'gy')), may hold values from -0.125 to 0.125
- tile_row: int32 [16384], P(('gx', 'gy')), may hold values from 0 to 511, as said below
- tile_col: int32 [16384], P(('gx', 'gy')), may hold values from 0 to 511, as said below
- tile_work: int32 [16384], P(('gx', 'gy')), may hold values from 0 to 16384, as said below
Outputs:
- product: float32 [65536, 128], P(('gx', 'gy'))
- moved_vals: bfloat16 [8192, 128, 128], P(('gx', 'gy'))
- moved_row: int32 [8192], P(('gx', 'gy'))
- moved_col: int32 [8192], P(('gx', 'gy'))
- moved_work: int32 [8192], P(('gx', 'gy'))
Inputs may be any that keep to these rules, and one draw needn't show every extreme that they name: `tile_work`: on every device the live slots come first; each gx row of 32 devices holds exactly 1024 live tiles, and in every row one device has all 64 slots live. `tile_row`: A tile held by device (a, b) has a row block owned by a device of gx index a. `tile_col`: A tile held by device (a, b) has a column block owned by a device of gy index b.
All inputs are finite; a program needn't handle non-finite values.
Results may differ from a plain program's by a relative error of at most 0.001.
Values may be sent and summed in bfloat16 or wider, within the bound.
A program may use at most 64 MiB of HBM per device.

v0:
```python
import jax
import jax.numpy as jnp
from jax import lax
from jax.sharding import Mesh
from jax.sharding import PartitionSpec as P

GY = ("gy_0", "gy_1")
GX_GY = ("gx", "gy_0", "gy_1")


def from_everyone(array, axis):
    copies = jnp.broadcast_to(array, (lax.axis_size(axis), *array.shape))
    return lax.all_to_all(copies, axis, split_axis=0, concat_axis=0, tiled=True)


def folded_in_pairs(pieces, combine):
    while len(jax.tree.leaves(pieces)[0]) > 1:
        pieces = jax.vmap(combine)(*(pieces[side::2] for side in (0, 1)))
    return pieces[0]


def carried_in(array, axis, combine, identity):
    count, position = (lax.axis_size(axis), lax.axis_index(axis))
    passed = jnp.arange(count) < position

    def kept(part, zero, own):
        part = jnp.where(
            passed.reshape(-1, *(1 for _ in own.shape)), part, jnp.asarray(zero, own.dtype)
        )
        return part

    pieces = from_everyone(array, axis)
    return folded_in_pairs(kept(pieces, identity, array), combine)


def in_order(tiles, dim):
    tiles = jnp.moveaxis(tiles, 0, dim)
    shape = tiles.shape
    return tiles.reshape(*shape[:dim], shape[dim] * shape[dim + 1], *shape[dim + 2 :])


def gathered_copies(array, axis, dim):
    tiles = from_everyone(array, axis)
    return in_order(tiles, dim)


def summed_rows(array, axes, dim):
    if not axes:
        return array
    nearer = lax.psum_scatter(array, axes[0], scatter_dimension=dim, tiled=True)
    return summed_rows(nearer, axes[1:], dim)


def add_counts(earlier, later):
    return earlier + later


def tile_products(values, work, vectors, pattern):
    masked = jnp.where(
        pattern[None, :, :] < work[:, None, None], values, jnp.zeros((), jnp.bfloat16)
    )
    return jnp.einsum("tij,tjk->tik", masked, vectors, preferred_element_type=jnp.float32)


def on_device(features, tile_vals, tile_row, tile_col, tile_work):
    peers = lax.axis_size(GY)
    slots = tile_vals.shape[0]
    share = slots // peers
    owned = slots // 2
    order = tile_vals.shape[1]
    width = features.shape[1]
    vblocks = features.shape[0] // order
    live = (tile_work > 0).astype(jnp.int32)
    count = jnp.sum(live)
    first = carried_in(count, GY, add_counts, jnp.int32(0))
    column_set = gathered_copies(features, "gx", 0).reshape(-1, order, width)
    column_pos = tile_col // vblocks // peers * vblocks + tile_col % vblocks
    row_base = lax.axis_index("gx") * peers * vblocks
    pattern = jnp.arange(order * order, dtype=jnp.int32).reshape(order, order)
    target_peer = jnp.arange(peers, dtype=jnp.int32)[:, None]
    within = jnp.arange(share, dtype=jnp.int32)[None, :]
    picked = (within * peers + (target_peer - first) % peers).reshape(-1)
    sent_row = jnp.take(tile_row, picked)
    sent_col = jnp.take(tile_col, picked)
    sent_work = jnp.take(tile_work, picked)
    sent_place = first + picked
    got_row, got_col, got_work, got_place = (
        lax.all_to_all(sent_row, GY, split_axis=0, concat_axis=0, tiled=True),
        lax.all_to_all(sent_col, GY, split_axis=0, concat_axis=0, tiled=True),
        lax.all_to_all(sent_work, GY, split_axis=0, concat_axis=0, tiled=True),
        lax.all_to_all(sent_place, GY, split_axis=0, concat_axis=0, tiled=True),
    )
    landing = (got_place - lax.axis_index(GY)) // peers
    matches = (landing[None, :] == jnp.arange(owned, dtype=jnp.int32)[:, None]) & (
        got_work[None, :] > 0
    )
    source_slot = jnp.argmax(matches, axis=1)
    moved_row = jnp.take(got_row, source_slot)
    moved_col = jnp.take(got_col, source_slot)
    moved_work = jnp.take(got_work, source_slot)
    vectors = jnp.take(column_set, column_pos, axis=0)
    products = tile_products(tile_vals, tile_work, vectors, pattern)
    row_local = tile_row - row_base
    sent_vals = jnp.take(tile_vals, picked, axis=0)
    got_vals = lax.all_to_all(sent_vals, GY, split_axis=0, concat_axis=0, tiled=True)
    moved_vals = jnp.take(got_vals, source_slot, axis=0)
    partial_value = jax.ops.segment_sum(products, row_local, num_segments=peers * vblocks).reshape(
        -1, width
    )
    summed = summed_rows(partial_value, GY, 0)
    return (summed, moved_vals, moved_row, moved_col, moved_work)


def solution(mesh):
    finer = Mesh(mesh.devices.reshape(mesh.shape["gx"], 4, 8), ("gx", "gy_0", "gy_1"))
    in_specs = (P(GX_GY, None), P(GX_GY, None, None), P(GX_GY), P(GX_GY), P(GX_GY))
    out_specs = (P(GX_GY, None), P(GX_GY, None, None), P(GX_GY), P(GX_GY), P(GX_GY))
    return jax.shard_map(
        on_device, mesh=finer, in_specs=in_specs, out_specs=out_specs, check_vma=False
    )
```

profile of v0, /device:TPU:32, one launch (start us, length us, event | category | flops | bytes accessed | tf_op | source)
XLA Modules:
  0.0 199.3 jit_solution(13350813140615190026)
XLA Ops:
  7.2 1.7 broadcast_in_dim.74
  8.9 4.3 %all-to-all-start = ((bf16[8,256,128]{2,1,0:T(8,128)(2,1)}), bf16[8,256,128]{2,1,0:T(8,128)(2,1)S(1)}, u32[]{:S(2)}, u32[]{:S(2)}) async-start(bf16[8,256,128]{2,1,0:T(8,128)(2,1)} %broadcast_in_dim.74), calls=%async_computation | async-start | bytes 1048576 | tf_op jit(solution)/shard_map/all_to_all | solution.py:13
  13.2 0.7 compare_and_fusion.2
  13.9 0.7 broadcast_subtract_fusion
  14.6 8.9 %all-to-all-done = bf16[8,256,128]{2,1,0:T(8,128)(2,1)S(1)} async-done(((bf16[8,256,128]{2,1,0:T(8,128)(2,1)}), bf16[8,256,128]{2,1,0:T(8,128)(2,1)S(1)}, u32[]{:S(2)}, u32[]{:S(2)}) %all-to-all-start) | async-done | bytes 524320 | tf_op jit(solution)/shard_map/all_to_all | solution.py:13
  23.5 2.1 %gather_fusion = bf16[64,128,128]{2,1,0:T(8,128)(2,1)} fusion(bf16[16,128,128]{2,1,0:T(8,128)(2,1)S(1)} %bitcast.12, s32[1024]{0:T(1024)S(1)} %pad_clamp_fusion.3), kind=kCustom, calls=%fused_computation.6 | custom fusion | bytes 4194560 | tf_op jit(solution)/shard_map/jit(_take)/gather | solution.py:101
  25.6 4.3 %fusion = f32[64,128,128]{2,1,0:T(8,128)} fusion(bf16[64,128,128]{2,1,0:T(8,128)(2,1)S(1)} %copy-done.3, bf16[64,128,128]{2,1,0:T(8,128)(2,1)} %gather_fusion, s32[128,128]{1,0:T(8,128)S(1)} %multiply_add_fusion, s32[64]{0:T(128)S(1)} %copy-done, pred[64]{0:T(512)(128)(4,1)S(1)} %get-tuple-element.13), kind=kOutput, calls=%fused_computation.11 | convolution fusion | flops 271581184 | bytes 8454464 | tf_op jit(solution)/shard_map/tij,tjk->tik/dot_general | solution.py:62
  30.0 2.5 %broadcast_in_dim.70 = f32[64,128,128]{2,1,0:T(8,128)} broadcast(f32[]{:T(128)} %constant.128.clone.1), dimensions={} | broadcast | bytes 4194308 | tf_op jit(solution)/shard_map/broadcast_in_dim | solution.py:107
  32.5 13.4 %scatter_fusion = f32[64,128,128]{2,1,0:T(8,128)} fusion(f32[64,128,128]{2,1,0:T(8,128)} %broadcast_in_dim.70, s32[64]{0:T(128)S(1)} %broadcast_subtract_fusion, f32[64,128,128]{2,1,0:T(8,128)} %fusion), kind=kCustom, calls=%fused_computation.9 | custom fusion | flops 1048576 | bytes 12583168 | tf_op jit(solution)/shard_map/scatter-add | solution.py:107
  45.9 0.6 fusion.9
  46.5 1.3 broadcast_in_dim.77
  47.8 11.3 %all-to-all-start.1 = ((s32[32,1,1]{2,1,0:T(1,128)}), s32[32,1,1]{2,1,0:T(1,128)S(1)}, u32[]{:S(2)}, u32[]{:S(2)}) async-start(s32[32,1,1]{2,1,0:T(1,128)} %broadcast_in_dim.77), calls=%async_computation.3 | async-start | bytes 32768 | tf_op jit(solution)/shard_map/all_to_all | solution.py:13
  59.1 8.6 %all-to-all-done.1 = s32[32,1,1]{2,1,0:T(1,128)S(1)} async-done(((s32[32,1,1]{2,1,0:T(1,128)}), s32[32,1,1]{2,1,0:T(1,128)S(1)}, u32[]{:S(2)}, u32[]{:S(2)}) %all-to-all-start.1) | async-done | bytes 160 | tf_op jit(solution)/shard_map/all_to_all | solution.py:13
  67.7 0.7 reduce.18
  68.4 0.1 slice.32
  69.2 0.6 fusion.14
  71.3 0.8 gather_fusion.6
  72.1 0.8 gather_fusion.4
  72.9 0.8 gather_fusion.3
  73.7 0.7 copy.19
  74.4 4.9 %all-to-all-start.2 = ((s32[32,2,1]{1,2,0:T(1,128)}), s32[32,2,1]{1,2,0:T(1,128)S(1)}, u32[]{:S(2)}, u32[]{:S(2)}) async-start(s32[32,2,1]{1,2,0:T(1,128)} %copy.19), calls=%async_computation.4 | async-start | bytes 32768 | tf_op jit(solution)/shard_map/all_to_all | solution.py:91
  79.5 0.7 all_to_all.44
  80.2 7.8 %all-to-all-done.2 = s32[32,2,1]{1,2,0:T(1,128)S(1)} async-done(((s32[32,2,1]{1,2,0:T(1,128)}), s32[32,2,1]{1,2,0:T(1,128)S(1)}, u32[]{:S(2)}, u32[]{:S(2)}) %all-to-all-start.2) | async-done | bytes 288 | tf_op jit(solution)/shard_map/all_to_all | solution.py:91
  88.0 4.9 %all-to-all-start.3 = ((s32[32,2,1]{1,2,0:T(1,128)}), s32[32,2,1]{1,2,0:T(1,128)S(1)}, u32[]{:S(2)}, u32[]{:S(2)}) async-start(s32[32,2,1]{1,2,0:T(1,128)} %bitcast.3), calls=%async_computation.5 | async-start | bytes 32768 | tf_op jit(solution)/shard_map/all_to_all | solution.py:90
  92.9 0.7 all_to_all.51
  93.6 8.0 %all-to-all-done.3 = s32[32,2,1]{1,2,0:T(1,128)S(1)} async-done(((s32[32,2,1]{1,2,0:T(1,128)}), s32[32,2,1]{1,2,0:T(1,128)S(1)}, u32[]{:S(2)}, u32[]{:S(2)}) %all-to-all-start.3) | async-done | bytes 288 | tf_op jit(solution)/shard_map/all_to_all | solution.py:90
  101.6 4.9 %all-to-all-start.6 = ((s32[32,2,1]{1,2,0:T(1,128)}), s32[32,2,1]{1,2,0:T(1,128)S(1)}, u32[]{:S(2)}, u32[]{:S(2)}) async-start(s32[32,2,1]{1,2,0:T(1,128)} %bitcast.6), calls=%async_computation.8 | async-start | bytes 32768 | tf_op jit(solution)/shard_map/all_to_all | solution.py:89
  106.5 2.1 %gather_fusion.1 = bf16[64,128,128]{2,1,0:T(8,128)(2,1)} fusion(bf16[64,128,128]{2,1,0:T(8,128)(2,1)S(1)} %copy-done.3, s32[1024]{0:T(1024)S(1)} %pad_clamp_fusion.1), kind=kCustom, calls=%fused_computation.7 | custom fusion | bytes 4194560 | tf_op jit(solution)/shard_map/jit(_take)/gather | solution.py:104
  108.6 0.7 all_to_all.48
  109.3 5.8 %all-to-all-done.6 = s32[32,2,1]{1,2,0:T(1,128)S(1)} async-done(((s32[32,2,1]{1,2,0:T(1,128)}), s32[32,2,1]{1,2,0:T(1,128)S(1)}, u32[]{:S(2)}, u32[]{:S(2)}) %all-to-all-start.6) | async-done | bytes 288 | tf_op jit(solution)/shard_map/all_to_all | solution.py:89
  115.2 4.9 %all-to-all-start.5 = ((s32[32,2,1]{1,2,0:T(1,128)}), s32[32,2,1]{1,2,0:T(1,128)S(1)}, u32[]{:S(2)}, u32[]{:S(2)}) async-start(s32[32,2,1]{1,2,0:T(1,128)} %bitcast.5), calls=%async_computation.7 | async-start | bytes 32768 | tf_op jit(solution)/shard_map/all_to_all | solution.py:88
  120.1 3.1 %broadcast_select_fusion = bf16[64,128,128]{2,1,0:T(8,128)(2,1)} fusion(bf16[64,128,128]{2,1,0:T(8,128)(2,1)} %gather_fusion.1, pred[64]{0:T(512)(128)(4,1)S(1)} %get-tuple-element.12), kind=kLoop, calls=%fused_computation.15 | loop fusion | flops 1048576 | bytes 4194368 | tf_op jit(solution)/shard_map/jit(_take)/select_n | solution.py:104
  123.2 5.5 %all-to-all-done.5 = s32[32,2,1]{1,2,0:T(1,128)S(1)} async-done(((s32[32,2,1]{1,2,0:T(1,128)}), s32[32,2,1]{1,2,0:T(1,128)S(1)}, u32[]{:S(2)}, u32[]{:S(2)}) %all-to-all-start.5) | async-done | bytes 288 | tf_op jit(solution)/shard_map/all_to_all | solution.py:88
  128.8 5.7 %all-to-all-start.4 = ((bf16[64,128,128]{2,1,0:T(8,128)(2,1)}), bf16[64,128,128]{2,1,0:T(8,128)(2,1)}, u32[]{:S(2)}, u32[]{:S(2)}) async-start(bf16[64,128,128]{2,1,0:T(8,128)(2,1)} %broadcast_select_fusion), calls=%async_computation.6 | async-start | bytes 4194304 | tf_op jit(solution)/shard_map/all_to_all | solution.py:105
  134.6 0.7 reduce-scatter.5.cloned.1.call-update
  135.4 0.5 broadcast.239
  135.9 0.7 reduce.33
  136.8 0.6 iota_reduce_fusion
  137.4 0.7 gather_fusion.8
  138.1 0.7 reduce.35
  138.9 0.7 gather_fusion.7
  139.6 0.7 reduce.34
  140.4 0.7 gather_fusion.5
  141.1 0.5 broadcast_select_fusion.2
  141.7 0.5 broadcast_select_fusion.3
  142.2 46.8 %all-to-all-done.4 = bf16[64,128,128]{2,1,0:T(8,128)(2,1)} async-done(((bf16[64,128,128]{2,1,0:T(8,128)(2,1)}), bf16[64,128,128]{2,1,0:T(8,128)(2,1)}, u32[]{:S(2)}, u32[]{:S(2)}) %all-to-all-start.4) | async-done | bytes 2097184 | tf_op jit(solution)/shard_map/all_to_all | solution.py:105
  189.0 2.3 %gather_fusion.2 = bf16[32,128,128]{2,1,0:T(8,128)(2,1)S(1)} fusion(bf16[64,128,128]{2,1,0:T(8,128)(2,1)} %all-to-all-done.4, s32[1024]{0:T(1024)S(1)} %pad_clamp_fusion), kind=kCustom, calls=%fused_computation.8 | custom fusion | bytes 2097280 | tf_op jit(solution)/shard_map/jit(_take)/gather | solution.py:106
  191.3 1.1 broadcast_select_fusion.1
  (48 shorter events, 1.7 us)
Async XLA Ops:
  8.9 14.6 %all-to-all-start = ((bf16[8,256,128]{2,1,0:T(8,128)(2,1)}), bf16[8,256,128]{2,1,0:T(8,128)(2,1)S(1)}, u32[]{:S(2)}, u32[]{:S(2)}) async-start(bf16[8,256,128]{2,1,0:T(8,128)(2,1)} %broadcast_in_dim.74), calls=%async_computation | async-start | bytes 1048576 | tf_op jit(solution)/shard_map/all_to_all | solution.py:13
  13.2 121.4 %reduce-scatter.3.cloned.1.call-start = ((), (), s32[]{:S(2)}) async-start(), calls=%async_computation.9 | async-start | bytes 5242880 | tf_op jit(solution)/shard_map/reduce_scatter | solution.py:50
  23.5 2.2 %copy-start = (s32[64]{0:T(128)S(1)}, s32[64]{0:T(128)}, u32[]{:S(2)}) copy-start(s32[64]{0:T(128)} %param.13) | copy-start | bytes 772
  23.5 2.2 %copy-start.3 = (bf16[64,128,128]{2,1,0:T(8,128)(2,1)S(1)}, bf16[64,128,128]{2,1,0:T(8,128)(2,1)}, u32[]{:S(2)}) copy-start(bf16[64,128,128]{2,1,0:T(8,128)(2,1)} %param.10) | copy-start | bytes 6291460
  45.9 25.4 %copy-start.1 = (s32[64]{0:T(128)S(1)}, s32[64]{0:T(128)}, u32[]{:S(2)}) copy-start(s32[64]{0:T(128)} %param.12) | copy-start | bytes 772
  45.9 26.2 %copy-start.2 = (s32[64]{0:T(128)S(1)}, s32[64]{0:T(128)}, u32[]{:S(2)}) copy-start(s32[64]{0:T(128)} %param.11) | copy-start | bytes 772
  47.8 19.9 %all-to-all-start.1 = ((s32[32,1,1]{2,1,0:T(1,128)}), s32[32,1,1]{2,1,0:T(1,128)S(1)}, u32[]{:S(2)}, u32[]{:S(2)}) async-start(s32[32,1,1]{2,1,0:T(1,128)} %broadcast_in_dim.77), calls=%async_computation.3 | async-start | bytes 32768 | tf_op jit(solution)/shard_map/all_to_all | solution.py:13
  74.4 13.6 %all-to-all-start.2 = ((s32[32,2,1]{1,2,0:T(1,128)}), s32[32,2,1]{1,2,0:T(1,128)S(1)}, u32[]{:S(2)}, u32[]{:S(2)}) async-start(s32[32,2,1]{1,2,0:T(1,128)} %copy.19), calls=%async_computation.4 | async-start | bytes 32768 | tf_op jit(solution)/shard_map/all_to_all | solution.py:91
  88.0 13.6 %all-to-all-start.3 = ((s32[32,2,1]{1,2,0:T(1,128)}), s32[32,2,1]{1,2,0:T(1,128)S(1)}, u32[]{:S(2)}, u32[]{:S(2)}) async-start(s32[32,2,1]{1,2,0:T(1,128)} %bitcast.3), calls=%async_computation.5 | async-start | bytes 32768 | tf_op jit(solution)/shard_map/all_to_all | solution.py:90
  101.6 13.6 %all-to-all-start.6 = ((s32[32,2,1]{1,2,0:T(1,128)}), s32[32,2,1]{1,2,0:T(1,128)S(1)}, u32[]{:S(2)}, u32[]{:S(2)}) async-start(s32[32,2,1]{1,2,0:T(1,128)} %bitcast.6), calls=%async_computation.8 | async-start | bytes 32768 | tf_op jit(solution)/shard_map/all_to_all | solution.py:89
  115.2 13.6 %all-to-all-start.5 = ((s32[32,2,1]{1,2,0:T(1,128)}), s32[32,2,1]{1,2,0:T(1,128)S(1)}, u32[]{:S(2)}, u32[]{:S(2)}) async-start(s32[32,2,1]{1,2,0:T(1,128)} %bitcast.5), calls=%async_computation.7 | async-start | bytes 32768 | tf_op jit(solution)/shard_map/all_to_all | solution.py:88
  128.8 60.2 %all-to-all-start.4 = ((bf16[64,128,128]{2,1,0:T(8,128)(2,1)}), bf16[64,128,128]{2,1,0:T(8,128)(2,1)}, u32[]{:S(2)}, u32[]{:S(2)}) async-start(bf16[64,128,128]{2,1,0:T(8,128)(2,1)} %broadcast_select_fusion), calls=%async_computation.6 | async-start | bytes 4194304 | tf_op jit(solution)/shard_map/all_to_all | solution.py:105
  134.5 57.9 %reduce-scatter.5.cloned.1.call-start = ((), (), s32[]{:S(2)}) async-start(), calls=%async_computation.10 | async-start | bytes 1179648 | tf_op jit(solution)/shard_map/reduce_scatter | solution.py:50
Sparse Core Ops, SparseCore 0:
  46.0 50.5 reduce-scatter.2
  138.4 48.4 reduce-scatter.4
where the time goes:
time: 200 us; the launch traced here: 199 us
  waiting for transfers between devices  92.1 us (46%)
  starting transfers between devices  41 us (20%)
  other arithmetic  24.4 us (12%)
  local copies, waits for them, and re-layouts  21.8 us (11%)
  between operations  15.6 us (8%)
  matrix products  4.34 us (2%)
    all_to_all x1, waiting for transfers between devices, on_device(): lax.all_to_all(sent_vals, GY, split_axis=0, concat_axis=0, tiled=True)  46.8 us
    all_to_all x2, waiting for transfers between devices, from_everyone(): return lax.all_to_all(copies, axis, split_axis=0, concat_axis=0, tiled=True)  17.5 us
    all_to_all x2, starting transfers between devices, from_everyone(): return lax.all_to_all(copies, axis, split_axis=0, concat_axis=0, tiled=True)  15.6 us
    scatter-add x1, other arithmetic, on_device(): jax.ops.segment_sum(products, row_local, num_segments=peers * vblocks)  13.4 us
    all_to_all x1, waiting for transfers between devices, on_device(): lax.all_to_all(sent_work, GY, split_axis=0, concat_axis=0, tiled=True)  7.96 us
    all_to_all x1, waiting for transfers between devices, on_device(): lax.all_to_all(sent_place, GY, split_axis=0, concat_axis=0, tiled=True)  7.84 us
    all_to_all x1, waiting for transfers between devices, on_device(): lax.all_to_all(sent_col, GY, split_axis=0, concat_axis=0, tiled=True)  5.85 us
    all_to_all x1, starting transfers between devices, on_device(): lax.all_to_all(sent_vals, GY, split_axis=0, concat_axis=0, tiled=True)  5.75 us
  transfers between devices with their start and end apart: 9, of which 7 were waited for; matrix products, arithmetic and copies ran while one was open for 12% of the time, Pallas kernels for 0%

commit v1 on v0

v1 whole, which is shorter than its diff:
```python
import functools

import jax
import jax.numpy as jnp
from jax import lax
from jax.experimental import pallas as pl
from jax.experimental.pallas import tpu as pltpu
from jax.sharding import PartitionSpec as P

NZ = 8
PARTS = (10, 21)
LIMIT = 32000.0
TINY = 1e-30
MESH = pl.DeviceIdType.MESH


def near_first(count):
    return sorted(range(1, count), key=lambda d: (min(d, count - d), d))


def tile_routes(ny, nz):
    pairs = [(dy, dz) for dz in [0, *near_first(nz)] for dy in [0, *near_first(ny)]]
    return pairs[1:]


def whole_wait(ref, sem):
    pltpu.make_async_copy(ref, ref, sem).wait()


def narrowed(value):
    peak = jnp.maximum(jnp.max(jnp.abs(value), axis=0, keepdims=True), TINY)
    coded = jnp.round(value * (LIMIT / peak)).astype(jnp.int32).astype(jnp.int16)
    return coded, peak * (1.0 / LIMIT)


def widened(coded, scale):
    return coded.astype(jnp.int32).astype(jnp.float32) * scale


def kernel(
    sizes,
    feat,
    tiles_hbm,
    row_v,
    col_v,
    work_v,
    col_s,
    work_s,
    chain_s,
    prod,
    moved,
    mrow,
    mcol,
    mwork,
    tiles,
    sendbuf,
    recvbuf,
    xbuf,
    sums,
    metabuf,
    posbuf,
    rowbuf,
    colbuf,
    workbuf,
    yq,
    ys,
    yrecv,
    ysrecv,
    ysum,
    zq,
    zs,
    zrecv,
    zsrecv,
    source,
    sems,
):
    nx, ny, nz = sizes
    peers = ny * nz
    slots = tiles.shape[0]
    vb = feat.shape[0]
    per_row = peers * vb
    per_y = nz * vb
    gx, gy = lax.axis_index("gx"), lax.axis_index("gy")
    y, z = gy // nz, gy % nz
    (tile_in, meta_tx, meta_rx, feat_tx, feat_rx, vals_tx, vals_rx) = (sems.at[i] for i in range(7))
    (y_tx, y_rx, ys_tx, ys_rx, z_tx, z_rx, zs_tx, zs_rx) = (sems.at[7 + i] for i in range(8))

    load = pltpu.make_async_copy(tiles_hbm, tiles, tile_in)
    load.start()

    barrier = pltpu.get_barrier_semaphore()

    def greet_gy(d, carry):
        pl.semaphore_signal(barrier, inc=1, device_id={"gy": (gy + d) % peers}, device_id_type=MESH)
        return carry

    def greet_gx(d, carry):
        pl.semaphore_signal(barrier, inc=1, device_id={"gx": (gx + d) % nx}, device_id_type=MESH)
        return carry

    lax.fori_loop(1, peers, greet_gy, 0)
    lax.fori_loop(1, nx, greet_gx, 0)

    metabuf[gy] = jnp.zeros(metabuf.shape[1:], jnp.int32)
    metabuf[gy, 0:1, 0:slots] = row_v[...]
    metabuf[gy, 1:2, 0:slots] = col_v[...]
    metabuf[gy, 2:3, 0:slots] = work_v[...]
    live = jnp.sum((work_v[...] > 0).astype(jnp.int32), axis=1, keepdims=True)
    metabuf[gy, 3:4, :] = jnp.broadcast_to(live, (1, metabuf.shape[2]))
    xbuf[pl.ds(gx * vb, vb)] = feat[...]

    pl.semaphore_wait(barrier, peers - 1 + nx - 1)

    def send_meta(d, carry):
        pltpu.make_async_remote_copy(
            src_ref=metabuf.at[gy],
            dst_ref=metabuf.at[gy],
            send_sem=meta_tx,
            recv_sem=meta_rx,
            device_id={"gy": (gy + d) % peers},
            device_id_type=MESH,
        ).start()
        return carry

    lax.fori_loop(1, peers, send_meta, 0)

    def send_feat(d, carry):
        pltpu.make_async_remote_copy(
            src_ref=feat,
            dst_ref=xbuf.at[pl.ds(gx * vb, vb)],
            send_sem=feat_tx,
            recv_sem=feat_rx,
            device_id={"gx": (gx + d) % nx},
            device_id_type=MESH,
        ).start()
        return carry

    lax.fori_loop(1, nx, send_feat, 0)

    load.wait()
    whole_wait(metabuf.at[pl.ds(0, peers - 1)], meta_rx)

    def before(c, total):
        return total + jnp.where(c < gy, metabuf[c], 0)

    counted = lax.fori_loop(0, peers, before, jnp.zeros(metabuf.shape[1:], jnp.int32))
    first = jnp.max(counted[3:4, :])

    def arrange(t, carry):
        j = (t - first) & (peers - 1)
        sendbuf[2 * t] = tiles[j]
        sendbuf[2 * t + 1] = tiles[j + peers]
        return carry

    lax.fori_loop(0, peers, arrange, 0)

    routes = tile_routes(ny, nz)

    def send_tiles(begin, end):
        for dy, dz in routes[begin:end]:
            to = (y + dy) % ny * nz + (z + dz) % nz
            pltpu.make_async_remote_copy(
                src_ref=sendbuf.at[pl.ds(2 * to, 2)],
                dst_ref=recvbuf.at[pl.ds(2 * gy, 2)],
                send_sem=vals_tx,
                recv_sem=vals_rx,
                device_id={"gy": to},
                device_id_type=MESH,
            ).start()

    recvbuf[pl.ds(2 * gy, 2)] = sendbuf[pl.ds(2 * gy, 2)]
    cuts = [len(routes) * c // 31 for c in PARTS]
    send_tiles(0, cuts[0])

    whole_wait(xbuf.at[pl.ds(0, (nx - 1) * vb)], feat_rx)
    order = tiles.shape[1]
    pattern = lax.broadcasted_iota(jnp.int32, (order, order), 0) * order + lax.broadcasted_iota(
        jnp.int32, (order, order), 1
    )

    def multiply(t, carry):
        col = col_s[t]
        at = col // per_row * vb + col % vb
        kept = jnp.where(pattern < work_s[t], tiles[t].astype(jnp.float32), 0.0)
        sums[t] = jnp.dot(
            kept.astype(jnp.bfloat16), xbuf[at], preferred_element_type=jnp.float32
        )
        return carry

    lax.fori_loop(0, slots, multiply, 0, unroll=4)

    def chain(t, carry):
        prev = chain_s[t]
        sums[t] = sums[t] + jnp.where(prev >= 0, sums[jnp.maximum(prev, 0)], 0.0)
        return carry

    lax.fori_loop(0, slots, chain, 0)

    def partial(r):
        last = chain_s[slots + r]
        return jnp.where(last >= 0, sums[jnp.maximum(last, 0)], 0.0)

    def send_y(dy):
        to = (y + dy) % ny * nz + z
        for src, dst, tx, rx in ((yq, yrecv, y_tx, y_rx), (ys, ysrecv, ys_tx, ys_rx)):
            pltpu.make_async_remote_copy(
                src_ref=src.at[dy - 1],
                dst_ref=dst.at[dy - 1],
                send_sem=tx,
                recv_sem=rx,
                device_id={"gy": to},
                device_id_type=MESH,
            ).start()

    for dy in range(1, ny):
        base = (y + dy) % ny * per_y

        def code_y(k, carry, dy=dy, base=base):
            coded, scale = narrowed(partial(base + k))
            yq[dy - 1, k] = coded
            ys[dy - 1, pl.ds(k, 1), :] = scale
            return carry

        lax.fori_loop(0, per_y, code_y, 0, unroll=2)
        if dy > 1:
            send_y(dy - 1)

    def own_y(k, carry):
        ysum[k] = partial(y * per_y + k)
        return carry

    lax.fori_loop(0, per_y, own_y, 0)
    send_y(ny - 1)
    send_tiles(cuts[0], cuts[1])

    whole_wait(yrecv, y_rx)
    whole_wait(ysrecv, ys_rx)

    def add_y(k, carry):
        total = ysum[k]
        for dy in range(1, ny):
            total = total + widened(yrecv[dy - 1, k], ysrecv[dy - 1, pl.ds(k, 1), :])
        ysum[k] = total
        return carry

    lax.fori_loop(0, per_y, add_y, 0)

    def send_z(dz):
        to = y * nz + (z + dz) % nz
        for src, dst, tx, rx in ((zq, zrecv, z_tx, z_rx), (zs, zsrecv, zs_tx, zs_rx)):
            pltpu.make_async_remote_copy(
                src_ref=src.at[dz - 1],
                dst_ref=dst.at[dz - 1],
                send_sem=tx,
                recv_sem=rx,
                device_id={"gy": to},
                device_id_type=MESH,
            ).start()

    def code_z(i, carry):
        dz, v = i // vb + 1, i % vb
        coded, scale = narrowed(ysum[(z + dz) % nz * vb + v])
        zq[dz - 1, v] = coded
        zs[dz - 1, pl.ds(v, 1), :] = scale
        return carry

    lax.fori_loop(0, (nz - 1) * vb, code_z, 0, unroll=2)
    for v in range(vb):
        prod[v] = ysum[z * vb + v]
    for dz in near_first(nz)[::-1]:
        send_z(dz)
    send_tiles(cuts[1], len(routes))

    lane = lax.broadcasted_iota(jnp.int32, (1, posbuf.shape[1]), 1)
    offset = jnp.zeros((1, posbuf.shape[1]), jnp.int32)
    for c in range(peers):
        one = metabuf[c]
        rowbuf[c : c + 1, :] = one[0:1, :]
        colbuf[c : c + 1, :] = one[1:2, :]
        workbuf[c : c + 1, :] = one[2:3, :]
        posbuf[c : c + 1, :] = jnp.where(one[2:3, :] > 0, offset + lane, -1)
        offset = offset + one[3:4, :]

    lanes = posbuf.shape
    origin = 2 * lax.broadcasted_iota(jnp.int32, lanes, 0) + (
        lax.broadcasted_iota(jnp.int32, lanes, 1) >= peers
    ).astype(jnp.int32)

    def place(q, carry):
        hit = posbuf[...] == q * peers + gy

        def picked(values):
            return jnp.sum(jnp.where(hit, values, 0))

        mrow[q] = picked(rowbuf[...])
        mcol[q] = picked(colbuf[...])
        mwork[q] = picked(workbuf[...])
        source[q] = picked(origin)
        return carry

    lax.fori_loop(0, slots // 2, place, 0)

    whole_wait(zrecv, z_rx)
    whole_wait(zsrecv, zs_rx)
    for v in range(vb):

        def add_z(d, total, v=v):
            return total + widened(zrecv[d, v], zsrecv[d, v : v + 1, :])

        prod[v] = lax.fori_loop(0, nz - 1, add_z, prod[v])

    whole_wait(recvbuf.at[pl.ds(0, 2 * (peers - 1))], vals_rx)

    def settle(q, carry):
        moved[q] = jnp.where(mwork[q] > 0, recvbuf[source[q]].astype(jnp.float32), 0.0).astype(
            moved.dtype
        )
        return carry

    lax.fori_loop(0, slots // 2, settle, 0, unroll=2)

    whole_wait(metabuf.at[pl.ds(0, peers - 1)], meta_tx)
    whole_wait(xbuf.at[pl.ds(0, (nx - 1) * vb)], feat_tx)
    whole_wait(recvbuf.at[pl.ds(0, 2 * (peers - 1))], vals_tx)
    whole_wait(yrecv, y_tx)
    whole_wait(ysrecv, ys_tx)
    whole_wait(zrecv, z_tx)
    whole_wait(zsrecv, zs_tx)


def on_device(sizes, features, tile_vals, tile_row, tile_col, tile_work):
    nx, ny, nz = sizes
    peers = ny * nz
    slots, order, _ = tile_vals.shape
    width = features.shape[1]
    vb = features.shape[0] // order
    local = tile_row - lax.axis_index("gx") * peers * vb
    index = jnp.arange(slots, dtype=jnp.int32)
    wanted = jnp.concatenate([local, jnp.arange(peers * vb, dtype=jnp.int32)])
    until = jnp.concatenate([index, jnp.full((peers * vb,), slots, jnp.int32)])
    found = (wanted[:, None] == local[None, :]) & (index[None, :] < until[:, None])
    chain = jnp.max(jnp.where(found, index[None, :], -1), axis=1)
    per_y = nz * vb
    bf16, f32, i32, i16 = jnp.bfloat16, jnp.float32, jnp.int32, jnp.int16
    vmem, smem = pltpu.VMEM, pltpu.SMEM
    in_vmem, in_smem = pl.BlockSpec(memory_space=vmem), pl.BlockSpec(memory_space=smem)
    prod, moved, mrow, mcol, mwork = pl.pallas_call(
        functools.partial(kernel, sizes),
        out_shape=(
            jax.ShapeDtypeStruct((vb, order, width), f32),
            jax.ShapeDtypeStruct((slots // 2, order, order), bf16),
            *[jax.ShapeDtypeStruct((slots // 2,), i32)] * 3,
        ),
        in_specs=[
            in_vmem,
            pl.BlockSpec(memory_space=pl.ANY),
            in_vmem,
            in_vmem,
            in_vmem,
            in_smem,
            in_smem,
            in_smem,
        ],
        out_specs=(in_vmem, in_vmem, in_smem, in_smem, in_smem),
        scratch_shapes=[
            vmem((slots, order, order), bf16),
            vmem((slots, order, order), bf16),
            vmem((slots, order, order), bf16),
            vmem((nx * vb, order, width), bf16),
            vmem((slots, order, width), f32),
            vmem((peers, 8, 128), i32),
            *[vmem((peers, 128), i32)] * 4,
            vmem((ny - 1, per_y, order, width), i16),
            vmem((ny - 1, per_y, width), f32),
            vmem((ny - 1, per_y, order, width), i16),
            vmem((ny - 1, per_y, width), f32),
            vmem((per_y, order, width), f32),
            vmem((nz - 1, vb, order, width), i16),
            vmem((nz - 1, 8, width), f32),
            vmem((nz - 1, vb, order, width), i16),
            vmem((nz - 1, 8, width), f32),
            smem((slots // 2,), i32),
            pltpu.SemaphoreType.DMA((15,)),
        ],
        compiler_params=pltpu.CompilerParams(
            collective_id=0, has_side_effects=True, vmem_limit_bytes=40 * 2**20
        ),
    )(
        features.reshape(vb, order, width),
        tile_vals,
        tile_row.reshape(1, slots),
        tile_col.reshape(1, slots),
        tile_work.reshape(1, slots),
        tile_col,
        tile_work,
        chain,
    )
    return prod.reshape(vb * order, width), moved, mrow, mcol, mwork


def solution(mesh):
    nx, peers = mesh.shape["gx"], mesh.shape["gy"]
    nz = min(NZ, peers // 2)
    both = ("gx", "gy")
    specs = (P(both, None), P(both, None, None), P(both), P(both), P(both))
    return jax.shard_map(
        functools.partial(on_device, (nx, peers // nz, nz)),
        mesh=mesh,
        in_specs=specs,
        out_specs=specs,
        check_vma=False,
    )
```

time: 200 us -> 114 us (0.57)
  Pallas kernels: 0 us -> 104 us
  waiting for transfers between devices: 92.1 us -> 0 us
  starting transfers between devices: 41 us -> 0 us
  other arithmetic: 24.4 us -> 1.48 us
  between operations: 15.6 us -> 0.66 us
  local copies, waits for them, and re-layouts: 21.8 us -> 7.55 us
  matrix products: 4.34 us -> 0 us
    pallas_call x0 -> x1, Pallas kernels: none -> 104 us  [on_device(): pl.pallas_call(functools.partial(kernel, sizes), out_shape=(jax.ShapeDtyp...]
    all_to_all x7 -> x0, waiting for transfers between devices: 91.4 us -> none  [the longest x1 46.8 us: on_device(): lax.all_to_all(sent_vals, GY, split_axis=0, concat_axis=0, tiled=True)]
    all_to_all x7 -> x0, starting transfers between devices: 40.9 us -> none  [the longest x2 15.6 us: from_everyone(): return lax.all_to_all(copies, axis, split_axis=0, concat_axis=0, tiled=True)]
    scatter-add x1 -> x0, other arithmetic: 13.4 us -> none  [on_device(): jax.ops.segment_sum(products, row_local, num_segments=peers * vblocks)]
    gather x9 -> x0, local copies, waits for them, and re-layouts: 11 us -> none  [the longest x1 2.34 us: on_device(): moved_vals = jnp.take(got_vals, source_slot, axis=0)]
    unnamed x8 -> x15, local copies, waits for them, and re-layouts: 0.01 us -> 7.55 us
    broadcast_in_dim x3 -> x0, local copies, waits for them, and re-layouts: 5.44 us -> none  [the longest x2 2.96 us: from_everyone(): copies = jnp.broadcast_to(array, (lax.axis_size(axis), *array.shape))]
    select_n x12 -> x0, other arithmetic: 5.37 us -> none  [the longest x2 3.14 us: on_device(): sent_vals = jnp.take(tile_vals, picked, axis=0)]
  transfers between devices with their start and end apart: 9 -> 0, of which waited for: 7 -> 0; matrix products, arithmetic and copies ran while one was open for 12% -> 0% of each run, Pallas kernels for 0% -> 0%
where the time goes in v1:
time: 114 us
  Pallas kernels  104 us (91%)
  local copies, waits for them, and re-layouts  7.55 us (7%)
  other arithmetic  1.48 us (1%)
    pallas_call x1, Pallas kernels, on_device(): pl.pallas_call(functools.partial(kernel, sizes), out_shape=(jax.ShapeDtyp...  104 us
    unnamed x15, local copies, waits for them, and re-layouts  7.55 us

profile of v1, /device:TPU:32, one launch (start us, length us, event | category | flops | bytes accessed | tf_op | source)
XLA Modules:
  0.0 113.8 jit_solution(15050913571120076816)
XLA Ops:
  0.6 0.7 broadcast_subtract_fusion
  1.3 0.1 pad_add_fusion
  1.4 0.7 select_reduce_fusion.chain_s
  2.1 0.0 copy-start
  2.1 1.6 %copy-done = bf16[64,128,128]{2,1,0:T(8,128)(2,1)S(1)} copy-done((bf16[64,128,128]{2,1,0:T(8,128)(2,1)S(1)}, bf16[64,128,128]{2,1,0:T(8,128)(2,1)}, u32[]{:S(2)}) %copy-start) | copy-done | bytes 2097176
  3.7 0.0 copy-start.1
  3.7 0.8 copy-done.1
  4.6 0.0 copy-start.2
  4.6 0.7 copy-done.2
  5.2 0.0 copy-start.3
  5.2 0.7 copy-done.3
  5.9 0.0 copy-start.4
  5.9 0.7 copy-done.4
  6.5 104.1 %shard_map.92 = (f32[2,128,128]{2,1,0:T(8,128)S(1)}, bf16[32,128,128]{2,1,0:T(8,128)(2,1)S(1)}, s32[32]{0:T(128)S(1)}, s32[32]{0:T(128)S(1)}, s32[32]{0:T(128)S(1)}) custom-call(bf16[2,128,128]{2,1,0:T(8,128)(2,1)S(1)} %bitcast.6, bf16[64,128,128]{2,1,0:T(8,128)(2,1)S(1)} %copy-done, s32[1,64]{1,0:T(1,128)S(1)} %bitcast.9, s32[1,64]{1,0:T(1,128)S(1)} %bitcast.7, ...), custom_call_target="tpu_custom_call" | custom-call | tf_op jit(solution)/shard_map/pallas_call | solution.py:347
  110.6 0.7 copy.15
  111.2 1.0 copy.16
  112.2 0.5 copy.17
  112.7 0.5 copy.18
  113.2 0.5 copy.19
  (1 shorter events, 0.0 us)
Async XLA Ops:
  2.1 1.6 %copy-start = (bf16[64,128,128]{2,1,0:T(8,128)(2,1)S(1)}, bf16[64,128,128]{2,1,0:T(8,128)(2,1)}, u32[]{:S(2)}) copy-start(bf16[64,128,128]{2,1,0:T(8,128)(2,1)} %tiles_hbm.1) | copy-start | bytes 6291460
  3.7 0.8 copy-start.1
  4.6 0.7 copy-start.2
  5.2 0.7 copy-start.3
  5.9 0.7 copy-start.4

commit v2 on v1

--- a/solution.py
+++ b/solution.py
@@ -8,7 +8,7 @@
 from jax.sharding import PartitionSpec as P
 
 NZ = 8
-PARTS = (10, 21)
+FIRST = 16
 LIMIT = 32000.0
 TINY = 1e-30
 MESH = pl.DeviceIdType.MESH
@@ -20,7 +20,7 @@
 
 def tile_routes(ny, nz):
     pairs = [(dy, dz) for dz in [0, *near_first(nz)] for dy in [0, *near_first(ny)]]
-    return pairs[1:]
+    return pairs[:0:-1]
 
 
 def whole_wait(ref, sem):
@@ -39,19 +39,27 @@
 
 def kernel(
     sizes,
-    feat,
+    feat_hbm,
     tiles_hbm,
-    row_v,
-    col_v,
-    work_v,
-    col_s,
-    work_s,
-    chain_s,
+    row_hbm,
+    col_hbm,
+    work_hbm,
+    row_line,
+    col_line,
+    work_line,
     prod,
     moved,
     mrow,
     mcol,
     mwork,
+    row_s,
+    col_s,
+    work_s,
+    chain_s,
+    row_v,
+    col_v,
+    work_v,
+    chain_v,
     tiles,
     sendbuf,
     recvbuf,
@@ -77,7 +85,7 @@
     nx, ny, nz = sizes
     peers = ny * nz
     slots = tiles.shape[0]
-    vb = feat.shape[0]
+    vb = feat_hbm.shape[0]
     per_row = peers * vb
     per_y = nz * vb
     gx, gy = lax.axis_index("gx"), lax.axis_index("gy")
@@ -85,6 +93,23 @@
     (tile_in, meta_tx, meta_rx, feat_tx, feat_rx, vals_tx, vals_rx) = (sems.at[i] for i in range(7))
     (y_tx, y_rx, ys_tx, ys_rx, z_tx, z_rx, zs_tx, zs_rx) = (sems.at[7 + i] for i in range(8))
 
+    own_x = xbuf.at[pl.ds(gx * vb, vb)]
+    small = [
+        pltpu.make_async_copy(src, dst, sems.at[15 + i])
+        for i, (src, dst) in enumerate(
+            (
+                (row_hbm, row_s),
+                (row_line, row_v),
+                (work_line, work_v),
+                (col_line, col_v),
+                (feat_hbm, own_x),
+                (col_hbm, col_s),
+                (work_hbm, work_s),
+            )
+        )
+    ]
+    for copy in small:
+        copy.start()
     load = pltpu.make_async_copy(tiles_hbm, tiles, tile_in)
     load.start()
 
@@ -101,13 +126,27 @@
     lax.fori_loop(1, peers, greet_gy, 0)
     lax.fori_loop(1, nx, greet_gx, 0)
 
+    for copy in small:
+        copy.wait()
     metabuf[gy] = jnp.zeros(metabuf.shape[1:], jnp.int32)
     metabuf[gy, 0:1, 0:slots] = row_v[...]
     metabuf[gy, 1:2, 0:slots] = col_v[...]
     metabuf[gy, 2:3, 0:slots] = work_v[...]
     live = jnp.sum((work_v[...] > 0).astype(jnp.int32), axis=1, keepdims=True)
     metabuf[gy, 3:4, :] = jnp.broadcast_to(live, (1, metabuf.shape[2]))
-    xbuf[pl.ds(gx * vb, vb)] = feat[...]
+
+    lane = lax.broadcasted_iota(jnp.int32, (1, chain_v.shape[1]), 1)
+    chain_v[...] = lane - slots
+    chain_v[0:1, 0:slots] = row_v[...] - gx * per_row
+    wanted = chain_v[...]
+    until = jnp.where(lane < slots, lane, slots)
+
+    def link(t, latest):
+        return jnp.where((wanted == row_s[t] - gx * per_row) & (t < until), t, latest)
+
+    chain_v[...] = lax.fori_loop(0, slots, link, jnp.full(lane.shape, -1, jnp.int32), unroll=4)
+    table = pltpu.make_async_copy(chain_v, chain_s, sems.at[22])
+    table.start()
 
     pl.semaphore_wait(barrier, peers - 1 + nx - 1)
 
@@ -126,8 +165,8 @@
 
     def send_feat(d, carry):
         pltpu.make_async_remote_copy(
-            src_ref=feat,
-            dst_ref=xbuf.at[pl.ds(gx * vb, vb)],
+            src_ref=own_x,
+            dst_ref=own_x,
             send_sem=feat_tx,
             recv_sem=feat_rx,
             device_id={"gx": (gx + d) % nx},
@@ -169,8 +208,9 @@
             ).start()
 
     recvbuf[pl.ds(2 * gy, 2)] = sendbuf[pl.ds(2 * gy, 2)]
-    cuts = [len(routes) * c // 31 for c in PARTS]
-    send_tiles(0, cuts[0])
+    cut = len(routes) * FIRST // 31
+    send_tiles(0, cut)
+    table.wait()
 
     whole_wait(xbuf.at[pl.ds(0, (nx - 1) * vb)], feat_rx)
     order = tiles.shape[1]
@@ -190,14 +230,14 @@
     lax.fori_loop(0, slots, multiply, 0, unroll=4)
 
     def chain(t, carry):
-        prev = chain_s[t]
+        prev = chain_s[0, t]
         sums[t] = sums[t] + jnp.where(prev >= 0, sums[jnp.maximum(prev, 0)], 0.0)
         return carry
 
     lax.fori_loop(0, slots, chain, 0)
 
     def partial(r):
-        last = chain_s[slots + r]
+        last = chain_s[0, slots + r]
         return jnp.where(last >= 0, sums[jnp.maximum(last, 0)], 0.0)
 
     def send_y(dy):
@@ -231,7 +271,7 @@
 
     lax.fori_loop(0, per_y, own_y, 0)
     send_y(ny - 1)
-    send_tiles(cuts[0], cuts[1])
+    send_tiles(cut, len(routes))
 
     whole_wait(yrecv, y_rx)
     whole_wait(ysrecv, ys_rx)
@@ -269,9 +309,7 @@
         prod[v] = ysum[z * vb + v]
     for dz in near_first(nz)[::-1]:
         send_z(dz)
-    send_tiles(cuts[1], len(routes))
-
-    lane = lax.broadcasted_iota(jnp.int32, (1, posbuf.shape[1]), 1)
+
     offset = jnp.zeros((1, posbuf.shape[1]), jnp.int32)
     for c in range(peers):
         one = metabuf[c]
@@ -334,12 +372,6 @@
     slots, order, _ = tile_vals.shape
     width = features.shape[1]
     vb = features.shape[0] // order
-    local = tile_row - lax.axis_index("gx") * peers * vb
-    index = jnp.arange(slots, dtype=jnp.int32)
-    wanted = jnp.concatenate([local, jnp.arange(peers * vb, dtype=jnp.int32)])
-    until = jnp.concatenate([index, jnp.full((peers * vb,), slots, jnp.int32)])
-    found = (wanted[:, None] == local[None, :]) & (index[None, :] < until[:, None])
-    chain = jnp.max(jnp.where(found, index[None, :], -1), axis=1)
     per_y = nz * vb
     bf16, f32, i32, i16 = jnp.bfloat16, jnp.float32, jnp.int32, jnp.int16
     vmem, smem = pltpu.VMEM, pltpu.SMEM
@@ -351,18 +383,13 @@
             jax.ShapeDtypeStruct((slots // 2, order, order), bf16),
             *[jax.ShapeDtypeStruct((slots // 2,), i32)] * 3,
         ),
-        in_specs=[
-            in_vmem,
-            pl.BlockSpec(memory_space=pl.ANY),
-            in_vmem,
-            in_vmem,
-            in_vmem,
-            in_smem,
-            in_smem,
-            in_smem,
-        ],
+        in_specs=[pl.BlockSpec(memory_space=pltpu.HBM)] * 8,
         out_specs=(in_vmem, in_vmem, in_smem, in_smem, in_smem),
         scratch_shapes=[
+            *[smem((slots,), i32)] * 3,
+            smem((1, slots + peers * vb), i32),
+            *[vmem((1, slots), i32)] * 3,
+            vmem((1, slots + peers * vb), i32),
             vmem((slots, order, order), bf16),
             vmem((slots, order, order), bf16),
             vmem((slots, order, order), bf16),
@@ -380,20 +407,20 @@
             vmem((nz - 1, vb, order, width), i16),
             vmem((nz - 1, 8, width), f32),
             smem((slots // 2,), i32),
-            pltpu.SemaphoreType.DMA((15,)),
+            pltpu.SemaphoreType.DMA((23,)),
         ],
         compiler_params=pltpu.CompilerParams(
-            collective_id=0, has_side_effects=True, vmem_limit_bytes=40 * 2**20
+            collective_id=0, has_side_effects=True, vmem_limit_bytes=67043328
         ),
     )(
         features.reshape(vb, order, width),
         tile_vals,
+        tile_row,
+        tile_col,
+        tile_work,
         tile_row.reshape(1, slots),
         tile_col.reshape(1, slots),
         tile_work.reshape(1, slots),
-        tile_col,
-        tile_work,
-        chain,
     )
     return prod.reshape(vb * order, width), moved, mrow, mcol, mwork
 

time: 114 us -> 90.5 us (0.79); the launches traced: 114 us -> 88.8 us
  Pallas kernels: 104 us -> 82.7 us
  local copies, waits for them, and re-layouts: 7.55 us -> 5.42 us
  other arithmetic: 1.48 us -> 0 us
    pallas_call x1, Pallas kernels: 104 us -> 82.7 us  [on_device(): pl.pallas_call(functools.partial(kernel, sizes), out_shape=(jax.ShapeDtyp...]
    unnamed x15 -> x11, local copies, waits for them, and re-layouts: 7.55 us -> 5.42 us
where the time goes in v2:
time: 90.5 us; the launch traced here: 88.8 us
  Pallas kernels  82.7 us (91%)
  local copies, waits for them, and re-layouts  5.42 us (6%)
    pallas_call x1, Pallas kernels, on_device(): pl.pallas_call(functools.partial(kernel, sizes), out_shape=(jax.ShapeDtyp...  82.7 us
    unnamed x11, local copies, waits for them, and re-layouts  5.42 us

profile of v2, /device:TPU:32, one launch (start us, length us, event | category | flops | bytes accessed | tf_op | source)
XLA Modules:
  0.0 88.8 jit_solution(5832544191193333735)
XLA Ops:
  0.6 82.7 %shard_map.92 = (f32[2,128,128]{2,1,0:T(8,128)}, bf16[32,128,128]{2,1,0:T(8,128)(2,1)}, s32[32]{0:T(128)}, s32[32]{0:T(128)}, s32[32]{0:T(128)}) custom-call(bf16[2,128,128]{2,1,0:T(8,128)(2,1)} %bitcast.6, bf16[64,128,128]{2,1,0:T(8,128)(2,1)} %tiles_hbm.1, s32[64]{0:T(128)} %row_hbm.1, s32[64]{0:T(128)} %col_hbm.1, s32[64]{0:T(128)} %work_hbm.1, ...), custom_call_target="tpu_custom_call" | custom-call | tf_op jit(solution)/shard_map/pallas_call | solution.py:379
  83.3 0.0 copy-start.2
  83.3 0.0 copy-start.1
  83.3 0.0 copy-start
  83.3 1.6 %copy.15 = f32[256,128]{1,0:T(8,128)} copy(f32[256,128]{1,0:T(8,128)} %bitcast.5) | data formatting | bytes 262144
  84.9 2.3 %copy.16 = bf16[32,128,128]{2,1,0:T(8,128)(2,1)} copy(bf16[32,128,128]{2,1,0:T(8,128)(2,1)} %get-tuple-element.21) | data formatting | bytes 2097152
  87.2 0.0 copy-done.2
  87.2 0.5 copy.17
  87.7 0.0 copy-done.1
  87.7 0.5 copy.18
  88.3 0.0 copy-done
  88.3 0.5 copy.19
Async XLA Ops:
  83.3 3.9 %copy-start.2 = (s32[32]{0:T(128)S(1)}, s32[32]{0:T(128)}, u32[]{:S(2)}) copy-start(s32[32]{0:T(128)} %get-tuple-element.22) | copy-start | bytes 388
  83.3 4.4 %copy-start.1 = (s32[32]{0:T(128)S(1)}, s32[32]{0:T(128)}, u32[]{:S(2)}) copy-start(s32[32]{0:T(128)} %get-tuple-element.23) | copy-start | bytes 388
  83.3 4.9 %copy-start = (s32[32]{0:T(128)S(1)}, s32[32]{0:T(128)}, u32[]{:S(2)}) copy-start(s32[32]{0:T(128)} %get-tuple-element.24) | copy-start | bytes 388

commit v3 on v2

--- a/solution.py
+++ b/solution.py
@@ -8,7 +8,6 @@
 from jax.sharding import PartitionSpec as P
 
 NZ = 8
-FIRST = 16
 LIMIT = 32000.0
 TINY = 1e-30
 MESH = pl.DeviceIdType.MESH
@@ -19,8 +18,23 @@
 
 
 def tile_routes(ny, nz):
-    pairs = [(dy, dz) for dz in [0, *near_first(nz)] for dy in [0, *near_first(ny)]]
+    pairs = [(dy, dz) for dy in [0, *near_first(ny)] for dz in [0, *near_first(nz)]]
     return pairs[:0:-1]
+
+
+def z_groups(nz):
+    if nz < 8:
+        return [*near_first(nz)[::-1], 0]
+    return [4, 3, nz - 3, 1, nz - 1, 2, nz - 2, 0]
+
+
+def z_route(dz, nz):
+    hop = {3: 1, 4: 2, nz - 3: nz - 1}.get(dz, dz) if nz == 8 else dz
+    return hop, dz - 1
+
+
+def collected(dz, nz):
+    return {2: (4, 3), nz - 2: (nz - 3,)}.get(dz, ()) if nz == 8 else ()
 
 
 def whole_wait(ref, sem):
@@ -74,13 +88,16 @@
     ys,
     yrecv,
     ysrecv,
-    ysum,
     zq,
     zs,
     zrecv,
     zsrecv,
     source,
     sems,
+    y_tx,
+    y_rx,
+    z_tx,
+    z_rx,
 ):
     nx, ny, nz = sizes
     peers = ny * nz
@@ -91,11 +108,10 @@
     gx, gy = lax.axis_index("gx"), lax.axis_index("gy")
     y, z = gy // nz, gy % nz
     (tile_in, meta_tx, meta_rx, feat_tx, feat_rx, vals_tx, vals_rx) = (sems.at[i] for i in range(7))
-    (y_tx, y_rx, ys_tx, ys_rx, z_tx, z_rx, zs_tx, zs_rx) = (sems.at[7 + i] for i in range(8))
 
     own_x = xbuf.at[pl.ds(gx * vb, vb)]
     small = [
-        pltpu.make_async_copy(src, dst, sems.at[15 + i])
+        pltpu.make_async_copy(src, dst, sems.at[7 + i])
         for i, (src, dst) in enumerate(
             (
                 (row_hbm, row_s),
@@ -145,7 +161,7 @@
         return jnp.where((wanted == row_s[t] - gx * per_row) & (t < until), t, latest)
 
     chain_v[...] = lax.fori_loop(0, slots, link, jnp.full(lane.shape, -1, jnp.int32), unroll=4)
-    table = pltpu.make_async_copy(chain_v, chain_s, sems.at[22])
+    table = pltpu.make_async_copy(chain_v, chain_s, sems.at[14])
     table.start()
 
     pl.semaphore_wait(barrier, peers - 1 + nx - 1)
@@ -195,23 +211,21 @@
 
     routes = tile_routes(ny, nz)
 
-    def send_tiles(begin, end):
-        for dy, dz in routes[begin:end]:
-            to = (y + dy) % ny * nz + (z + dz) % nz
-            pltpu.make_async_remote_copy(
-                src_ref=sendbuf.at[pl.ds(2 * to, 2)],
-                dst_ref=recvbuf.at[pl.ds(2 * gy, 2)],
-                send_sem=vals_tx,
-                recv_sem=vals_rx,
-                device_id={"gy": to},
-                device_id_type=MESH,
-            ).start()
+    def send_tiles(dy, dz):
+        to = (y + dy) % ny * nz + (z + dz) % nz
+        pltpu.make_async_remote_copy(
+            src_ref=sendbuf.at[pl.ds(2 * to, 2)],
+            dst_ref=recvbuf.at[pl.ds(2 * gy, 2)],
+            send_sem=vals_tx,
+            recv_sem=vals_rx,
+            device_id={"gy": to},
+            device_id_type=MESH,
+        ).start()
 
     recvbuf[pl.ds(2 * gy, 2)] = sendbuf[pl.ds(2 * gy, 2)]
-    cut = len(routes) * FIRST // 31
-    send_tiles(0, cut)
+    for dy, dz in routes:
+        send_tiles(dy, dz)
     table.wait()
-
     whole_wait(xbuf.at[pl.ds(0, (nx - 1) * vb)], feat_rx)
     order = tiles.shape[1]
     pattern = lax.broadcasted_iota(jnp.int32, (order, order), 0) * order + lax.broadcasted_iota(
@@ -240,76 +254,47 @@
         last = chain_s[0, slots + r]
         return jnp.where(last >= 0, sums[jnp.maximum(last, 0)], 0.0)
 
-    def send_y(dy):
-        to = (y + dy) % ny * nz + z
-        for src, dst, tx, rx in ((yq, yrecv, y_tx, y_rx), (ys, ysrecv, ys_tx, ys_rx)):
+    groups = z_groups(nz)
+
+    def send_piece(src, scales, dst, dst_scales, tx, rx, to):
+        for one, other, i in ((src, dst, 0), (scales, dst_scales, 1)):
             pltpu.make_async_remote_copy(
-                src_ref=src.at[dy - 1],
-                dst_ref=dst.at[dy - 1],
-                send_sem=tx,
-                recv_sem=rx,
+                src_ref=one,
+                dst_ref=other,
+                send_sem=tx.at[i],
+                recv_sem=rx.at[i],
                 device_id={"gy": to},
                 device_id_type=MESH,
             ).start()
 
-    for dy in range(1, ny):
-        base = (y + dy) % ny * per_y
-
-        def code_y(k, carry, dy=dy, base=base):
-            coded, scale = narrowed(partial(base + k))
-            yq[dy - 1, k] = coded
-            ys[dy - 1, pl.ds(k, 1), :] = scale
+    def send_y(g):
+        for dy in range(1, ny):
+            send_piece(
+                yq.at[g, dy - 1],
+                ys.at[g, dy - 1],
+                yrecv.at[g, dy - 1],
+                ysrecv.at[g, dy - 1],
+                y_tx,
+                y_rx.at[g],
+                (y + dy) % ny * nz + z,
+            )
+
+    for g, dz in enumerate(groups):
+        begin = (z + dz) % nz * vb
+
+        def code_y(i, carry, g=g, begin=begin):
+            dy, v = i // vb + 1, i % vb
+            coded, scale = narrowed(partial((y + dy) % ny * per_y + begin + v))
+            yq[g, dy - 1, v] = coded
+            ys[g, dy - 1, pl.ds(v, 1), :] = scale
             return carry
 
-        lax.fori_loop(0, per_y, code_y, 0, unroll=2)
-        if dy > 1:
-            send_y(dy - 1)
-
-    def own_y(k, carry):
-        ysum[k] = partial(y * per_y + k)
-        return carry
-
-    lax.fori_loop(0, per_y, own_y, 0)
-    send_y(ny - 1)
-    send_tiles(cut, len(routes))
-
-    whole_wait(yrecv, y_rx)
-    whole_wait(ysrecv, ys_rx)
-
-    def add_y(k, carry):
-        total = ysum[k]
-        for dy in range(1, ny):
-            total = total + widened(yrecv[dy - 1, k], ysrecv[dy - 1, pl.ds(k, 1), :])
-        ysum[k] = total
-        return carry
-
-    lax.fori_loop(0, per_y, add_y, 0)
-
-    def send_z(dz):
-        to = y * nz + (z + dz) % nz
-        for src, dst, tx, rx in ((zq, zrecv, z_tx, z_rx), (zs, zsrecv, zs_tx, zs_rx)):
-            pltpu.make_async_remote_copy(
-                src_ref=src.at[dz - 1],
-                dst_ref=dst.at[dz - 1],
-                send_sem=tx,
-                recv_sem=rx,
-                device_id={"gy": to},
-                device_id_type=MESH,
-            ).start()
-
-    def code_z(i, carry):
-        dz, v = i // vb + 1, i % vb
-        coded, scale = narrowed(ysum[(z + dz) % nz * vb + v])
-        zq[dz - 1, v] = coded
-        zs[dz - 1, pl.ds(v, 1), :] = scale
-        return carry
-
-    lax.fori_loop(0, (nz - 1) * vb, code_z, 0, unroll=2)
-    for v in range(vb):
-        prod[v] = ysum[z * vb + v]
-    for dz in near_first(nz)[::-1]:
-        send_z(dz)
-
+        lax.fori_loop(0, (ny - 1) * vb, code_y, 0, unroll=2)
+        if g:
+            send_y(g - 1)
+    send_y(len(groups) - 1)
+
+    lane = lax.broadcasted_iota(jnp.int32, (1, posbuf.shape[1]), 1)
     offset = jnp.zeros((1, posbuf.shape[1]), jnp.int32)
     for c in range(peers):
         one = metabuf[c]
@@ -338,32 +323,82 @@
 
     lax.fori_loop(0, slots // 2, place, 0)
 
-    whole_wait(zrecv, z_rx)
-    whole_wait(zsrecv, zs_rx)
-    for v in range(vb):
-
-        def add_z(d, total, v=v):
-            return total + widened(zrecv[d, v], zsrecv[d, v : v + 1, :])
-
-        prod[v] = lax.fori_loop(0, nz - 1, add_z, prod[v])
+    pending = []
+
+    def flush():
+        while pending:
+            hop, slot = pending.pop()
+            send_piece(
+                zq.at[slot],
+                zs.at[slot],
+                zrecv.at[slot],
+                zsrecv.at[slot],
+                z_tx,
+                z_rx.at[slot],
+                y * nz + (z + hop) % nz,
+            )
+
+    def arrived(slot):
+        whole_wait(zrecv.at[slot], z_rx.at[slot, 0])
+        whole_wait(zsrecv.at[slot], z_rx.at[slot, 1])
+
+    for g, dz in enumerate(groups):
+        hop, slot = z_route(dz, nz)
+        whole_wait(yrecv.at[g], y_rx.at[g, 0])
+        whole_wait(ysrecv.at[g], y_rx.at[g, 1])
+        extra = collected(dz, nz)
+        for other in extra:
+            arrived(z_route(other, nz)[1])
+        begin = y * per_y + (z + dz) % nz * vb
+        for v in range(vb):
+            total = partial(begin + v)
+            for dy in range(1, ny):
+                total = total + widened(yrecv[g, dy - 1, v], ysrecv[g, dy - 1, v : v + 1, :])
+            for other in extra:
+                at = z_route(other, nz)[1]
+                total = total + widened(zrecv[at, v], zsrecv[at, v : v + 1, :])
+            if dz == 0:
+                prod[v] = total
+            else:
+                coded, scale = narrowed(total)
+                zq[slot, v] = coded
+                zs[slot, v : v + 1, :] = scale
+        flush()
+        if dz:
+            pending.append((hop, slot))
+    flush()
+    for dz in groups:
+        hop, slot = z_route(dz, nz)
+        if dz and hop == dz:
+            arrived(slot)
+            for v in range(vb):
+                prod[v] = prod[v] + widened(zrecv[slot, v], zsrecv[slot, v : v + 1, :])
 
     whole_wait(recvbuf.at[pl.ds(0, 2 * (peers - 1))], vals_rx)
 
     def settle(q, carry):
-        moved[q] = jnp.where(mwork[q] > 0, recvbuf[source[q]].astype(jnp.float32), 0.0).astype(
-            moved.dtype
-        )
-        return carry
-
-    lax.fori_loop(0, slots // 2, settle, 0, unroll=2)
+        moved[q] = recvbuf[source[q]]
+        return carry
+
+    lax.fori_loop(0, slots // 2, settle, 0, unroll=4)
 
     whole_wait(metabuf.at[pl.ds(0, peers - 1)], meta_tx)
     whole_wait(xbuf.at[pl.ds(0, (nx - 1) * vb)], feat_tx)
     whole_wait(recvbuf.at[pl.ds(0, 2 * (peers - 1))], vals_tx)
-    whole_wait(yrecv, y_tx)
-    whole_wait(ysrecv, ys_tx)
-    whole_wait(zrecv, z_tx)
-    whole_wait(zsrecv, zs_tx)
+    whole_wait(yrecv, y_tx.at[0])
+    whole_wait(ysrecv, y_tx.at[1])
+    whole_wait(zrecv, z_tx.at[0])
+    whole_wait(zsrecv, z_tx.at[1])
+
+
+def deliver(*refs):
+    count = len(refs) // 2
+    outs, sems = refs[count : 2 * count], refs[-1]
+    copies = [pltpu.make_async_copy(refs[i], outs[i], sems.at[i]) for i in range(count)]
+    for copy in copies:
+        copy.start()
+    for copy in copies:
+        copy.wait()
 
 
 def on_device(sizes, features, tile_vals, tile_row, tile_col, tile_work):
@@ -376,13 +411,14 @@
     bf16, f32, i32, i16 = jnp.bfloat16, jnp.float32, jnp.int32, jnp.int16
     vmem, smem = pltpu.VMEM, pltpu.SMEM
     in_vmem, in_smem = pl.BlockSpec(memory_space=vmem), pl.BlockSpec(memory_space=smem)
-    prod, moved, mrow, mcol, mwork = pl.pallas_call(
+    shapes = (
+        jax.ShapeDtypeStruct((vb, order, width), f32),
+        jax.ShapeDtypeStruct((slots // 2, order, order), bf16),
+        *[jax.ShapeDtypeStruct((slots // 2,), i32)] * 3,
+    )
+    results = pl.pallas_call(
         functools.partial(kernel, sizes),
-        out_shape=(
-            jax.ShapeDtypeStruct((vb, order, width), f32),
-            jax.ShapeDtypeStruct((slots // 2, order, order), bf16),
-            *[jax.ShapeDtypeStruct((slots // 2,), i32)] * 3,
-        ),
+        out_shape=shapes,
         in_specs=[pl.BlockSpec(memory_space=pltpu.HBM)] * 8,
         out_specs=(in_vmem, in_vmem, in_smem, in_smem, in_smem),
         scratch_shapes=[
@@ -397,17 +433,20 @@
             vmem((slots, order, width), f32),
             vmem((peers, 8, 128), i32),
             *[vmem((peers, 128), i32)] * 4,
-            vmem((ny - 1, per_y, order, width), i16),
-            vmem((ny - 1, per_y, width), f32),
-            vmem((ny - 1, per_y, order, width), i16),
-            vmem((ny - 1, per_y, width), f32),
-            vmem((per_y, order, width), f32),
+            vmem((nz, ny - 1, vb, order, width), i16),
+            vmem((nz, ny - 1, 8, width), f32),
+            vmem((nz, ny - 1, vb, order, width), i16),
+            vmem((nz, ny - 1, 8, width), f32),
             vmem((nz - 1, vb, order, width), i16),
             vmem((nz - 1, 8, width), f32),
             vmem((nz - 1, vb, order, width), i16),
             vmem((nz - 1, 8, width), f32),
             smem((slots // 2,), i32),
-            pltpu.SemaphoreType.DMA((23,)),
+            pltpu.SemaphoreType.DMA((15,)),
+            pltpu.SemaphoreType.DMA((2,)),
+            pltpu.SemaphoreType.DMA((nz, 2)),
+            pltpu.SemaphoreType.DMA((2,)),
+            pltpu.SemaphoreType.DMA((nz - 1, 2)),
         ],
         compiler_params=pltpu.CompilerParams(
             collective_id=0, has_side_effects=True, vmem_limit_bytes=67043328
@@ -422,6 +461,13 @@
         tile_col.reshape(1, slots),
         tile_work.reshape(1, slots),
     )
+    prod, moved, mrow, mcol, mwork = pl.pallas_call(
+        deliver,
+        out_shape=shapes,
+        in_specs=[in_vmem, in_vmem, in_smem, in_smem, in_smem],
+        out_specs=[pl.BlockSpec(memory_space=pltpu.HBM)] * 5,
+        scratch_shapes=[pltpu.SemaphoreType.DMA((5,))],
+    )(*results)
     return prod.reshape(vb * order, width), moved, mrow, mcol, mwork
 
 

time: 90.5 us -> 77.4 us (0.86); the launches traced: 88.8 us -> 76.7 us
  Pallas kernels: 82.7 us -> 76.1 us
  local copies, waits for them, and re-layouts: 5.42 us -> 0 us
    pallas_call x1 -> x2, Pallas kernels: 82.7 us -> 76.1 us  [the longest x1 73.7 us: on_device(): pl.pallas_call(functools.partial(kernel, sizes), out_shape=shapes, in_spe...]
    unnamed x11 -> x0, local copies, waits for them, and re-layouts: 5.42 us -> none
where the time goes in v3:
time: 77.4 us; the launch traced here: 76.7 us
  Pallas kernels  76.1 us (98%)
    pallas_call x1, Pallas kernels, on_device(): pl.pallas_call(functools.partial(kernel, sizes), out_shape=shapes, in_spe...  73.7 us
    pallas_call x1, Pallas kernels, on_device(): pl.pallas_call(deliver, out_shape=shapes, in_specs=[in_vmem, in_vmem, in_...  2.4 us

profile of v3, /device:TPU:32, one launch (start us, length us, event | category | flops | bytes accessed | tf_op | source)
XLA Modules:
  0.0 76.7 jit_solution(9766810684220734167)
XLA Ops:
  0.6 73.7 %shard_map.92 = (f32[2,128,128]{2,1,0:T(8,128)}, bf16[32,128,128]{2,1,0:T(8,128)(2,1)}, s32[32]{0:T(128)}, s32[32]{0:T(128)}, s32[32]{0:T(128)}) custom-call(bf16[2,128,128]{2,1,0:T(8,128)(2,1)} %bitcast.5, bf16[64,128,128]{2,1,0:T(8,128)(2,1)} %tiles_hbm.1, s32[64]{0:T(128)} %row_hbm.1, s32[64]{0:T(128)} %col_hbm.1, s32[64]{0:T(128)} %work_hbm.1, ...), custom_call_target="tpu_custom_call" | custom-call | tf_op jit(solution)/shard_map/pallas_call | solution.py:419
  74.3 2.4 %shard_map.93 = (f32[2,128,128]{2,1,0:T(8,128)}, bf16[32,128,128]{2,1,0:T(8,128)(2,1)}, s32[32]{0:T(128)}, s32[32]{0:T(128)}, s32[32]{0:T(128)}) custom-call(f32[2,128,128]{2,1,0:T(8,128)} %get-tuple-element.15.refs_0_, bf16[32,128,128]{2,1,0:T(8,128)(2,1)} %get-tuple-element.16.refs_1_, s32[32]{0:T(128)} %get-tuple-element.17.refs_2_, ...), custom_call_target="tpu_custom_call" | custom-call | tf_op jit(solution)/shard_map/pallas_call | solution.py:464

commit v4 on v3

--- a/solution.py
+++ b/solution.py
@@ -8,6 +8,9 @@
 from jax.sharding import PartitionSpec as P
 
 NZ = 8
+UP = 16
+AFTERY = 8
+PER = 1
 LIMIT = 32000.0
 TINY = 1e-30
 MESH = pl.DeviceIdType.MESH
@@ -23,18 +26,28 @@
 
 
 def z_groups(nz):
-    if nz < 8:
-        return [*near_first(nz)[::-1], 0]
-    return [4, 3, nz - 3, 1, nz - 1, 2, nz - 2, 0]
-
-
-def z_route(dz, nz):
-    hop = {3: 1, 4: 2, nz - 3: nz - 1}.get(dz, dz) if nz == 8 else dz
-    return hop, dz - 1
-
-
-def collected(dz, nz):
-    return {2: (4, 3), nz - 2: (nz - 3,)}.get(dz, ()) if nz == 8 else ()
+    half = nz // 2
+    return [half, *[d for k in range(half - 1, 0, -1) for d in (nz - k, k)], 0]
+
+
+def z_sends(dz, nz, vb):
+    half = nz // 2
+    if dz == half:
+        return [(half, 1, 0, vb // 2), (0, nz - 1, vb // 2, vb - vb // 2)]
+    return [(dz, 1 if dz < half else nz - 1, 0, vb)] if dz else []
+
+
+def z_carried(dz, nz, vb):
+    half = nz // 2
+    steps = [dz + 1] if dz < half else []
+    steps += [(dz - 1) % nz] if dz > half or dz == 0 else []
+    found = []
+    for step in steps:
+        up = step == (dz + 1)
+        for slot, hop, begin, count in z_sends(step, nz, vb):
+            if (hop == 1) == up or nz == 2:
+                found.append((slot, begin, count))
+    return found if nz > 2 else found[:2]
 
 
 def whole_wait(ref, sem):
@@ -81,13 +94,13 @@
     sums,
     metabuf,
     posbuf,
-    rowbuf,
-    colbuf,
+    cellbuf,
     workbuf,
     yq,
     ys,
     yrecv,
     ysrecv,
+    ysum,
     zq,
     zs,
     zrecv,
@@ -108,6 +121,7 @@
     gx, gy = lax.axis_index("gx"), lax.axis_index("gy")
     y, z = gy // nz, gy % nz
     (tile_in, meta_tx, meta_rx, feat_tx, feat_rx, vals_tx, vals_rx) = (sems.at[i] for i in range(7))
+    pass_tx, pass_rx = sems.at[15], sems.at[16]
 
     own_x = xbuf.at[pl.ds(gx * vb, vb)]
     small = [
@@ -144,12 +158,11 @@
 
     for copy in small:
         copy.wait()
-    metabuf[gy] = jnp.zeros(metabuf.shape[1:], jnp.int32)
-    metabuf[gy, 0:1, 0:slots] = row_v[...]
-    metabuf[gy, 1:2, 0:slots] = col_v[...]
-    metabuf[gy, 2:3, 0:slots] = work_v[...]
     live = jnp.sum((work_v[...] > 0).astype(jnp.int32), axis=1, keepdims=True)
-    metabuf[gy, 3:4, :] = jnp.broadcast_to(live, (1, metabuf.shape[2]))
+    width = 2 * slots
+    metabuf[gy, :, 0:width] = jnp.concatenate([row_v[...], col_v[...]], axis=1)
+    metabuf[gy, :, width : 2 * width] = jnp.concatenate([work_v[...], work_v[...]], axis=1)
+    metabuf[gy, :, 2 * width : 3 * width] = jnp.broadcast_to(live, (1, width))
 
     lane = lax.broadcasted_iota(jnp.int32, (1, chain_v.shape[1]), 1)
     chain_v[...] = lane - slots
@@ -179,18 +192,23 @@
 
     lax.fori_loop(1, peers, send_meta, 0)
 
-    def send_feat(d, carry):
+    pair = gx // 2 * 2
+    partner = pair + 1 - gx % 2
+
+    def send_feat(block, to, tx, rx):
+        at = xbuf.at[pl.ds(block * vb, vb)]
         pltpu.make_async_remote_copy(
-            src_ref=own_x,
-            dst_ref=own_x,
-            send_sem=feat_tx,
-            recv_sem=feat_rx,
-            device_id={"gx": (gx + d) % nx},
+            src_ref=at,
+            dst_ref=at,
+            send_sem=tx,
+            recv_sem=rx,
+            device_id={"gx": to},
             device_id_type=MESH,
         ).start()
-        return carry
-
-    lax.fori_loop(1, nx, send_feat, 0)
+
+    for d in near_first(nx // 2)[::-1]:
+        send_feat(gx, (gx + 2 * d) % nx, feat_tx, feat_rx)
+    send_feat(gx, partner, feat_tx, pass_rx)
 
     load.wait()
     whole_wait(metabuf.at[pl.ds(0, peers - 1)], meta_rx)
@@ -199,15 +217,7 @@
         return total + jnp.where(c < gy, metabuf[c], 0)
 
     counted = lax.fori_loop(0, peers, before, jnp.zeros(metabuf.shape[1:], jnp.int32))
-    first = jnp.max(counted[3:4, :])
-
-    def arrange(t, carry):
-        j = (t - first) & (peers - 1)
-        sendbuf[2 * t] = tiles[j]
-        sendbuf[2 * t + 1] = tiles[j + peers]
-        return carry
-
-    lax.fori_loop(0, peers, arrange, 0)
+    first = jnp.max(counted[:, 2 * width : 3 * width])
 
     routes = tile_routes(ny, nz)
 
@@ -222,11 +232,29 @@
             device_id_type=MESH,
         ).start()
 
-    recvbuf[pl.ds(2 * gy, 2)] = sendbuf[pl.ds(2 * gy, 2)]
-    for dy, dz in routes:
-        send_tiles(dy, dz)
+    for i, (dy, dz) in enumerate(routes):
+        to = (y + dy) % ny * nz + (z + dz) % nz
+        j = (to - first) & (peers - 1)
+        sendbuf[2 * to] = tiles[j]
+        sendbuf[2 * to + 1] = tiles[j + peers]
+        if 0 < i <= UP:
+            send_tiles(*routes[i - 1])
+    own = (gy - first) & (peers - 1)
+    recvbuf[2 * gy] = tiles[own]
+    recvbuf[2 * gy + 1] = tiles[own + peers]
+    if UP >= len(routes):
+        send_tiles(*routes[-1])
+    held = list(routes[UP:])
+
+    def more(n):
+        for _ in range(min(n, len(held))):
+            send_tiles(*held.pop(0))
+
+    whole_wait(xbuf.at[pl.ds(0, (nx // 2 - 1) * vb)], feat_rx)
+    for d in range(1, nx // 2):
+        send_feat((gx + 2 * d) % nx, partner, pass_tx, pass_rx)
     table.wait()
-    whole_wait(xbuf.at[pl.ds(0, (nx - 1) * vb)], feat_rx)
+    whole_wait(xbuf.at[pl.ds(0, nx // 2 * vb)], pass_rx)
     order = tiles.shape[1]
     pattern = lax.broadcasted_iota(jnp.int32, (order, order), 0) * order + lax.broadcasted_iota(
         jnp.int32, (order, order), 1
@@ -236,19 +264,12 @@
         col = col_s[t]
         at = col // per_row * vb + col % vb
         kept = jnp.where(pattern < work_s[t], tiles[t].astype(jnp.float32), 0.0)
-        sums[t] = jnp.dot(
-            kept.astype(jnp.bfloat16), xbuf[at], preferred_element_type=jnp.float32
-        )
+        product = jnp.dot(kept.astype(jnp.bfloat16), xbuf[at], preferred_element_type=jnp.float32)
+        prev = chain_s[0, t]
+        sums[t] = product + jnp.where(prev >= 0, sums[jnp.maximum(prev, 0)], 0.0)
         return carry
 
     lax.fori_loop(0, slots, multiply, 0, unroll=4)
-
-    def chain(t, carry):
-        prev = chain_s[0, t]
-        sums[t] = sums[t] + jnp.where(prev >= 0, sums[jnp.maximum(prev, 0)], 0.0)
-        return carry
-
-    lax.fori_loop(0, slots, chain, 0)
 
     def partial(r):
         last = chain_s[0, slots + r]
@@ -293,87 +314,88 @@
         if g:
             send_y(g - 1)
     send_y(len(groups) - 1)
-
-    lane = lax.broadcasted_iota(jnp.int32, (1, posbuf.shape[1]), 1)
-    offset = jnp.zeros((1, posbuf.shape[1]), jnp.int32)
+    more(AFTERY)
+
+    lane = lax.broadcasted_iota(jnp.int32, (1, width), 1)
+    slot_of = jnp.where(lane < slots, lane, lane - slots)
+    offset = jnp.zeros((1, width), jnp.int32)
     for c in range(peers):
         one = metabuf[c]
-        rowbuf[c : c + 1, :] = one[0:1, :]
-        colbuf[c : c + 1, :] = one[1:2, :]
-        workbuf[c : c + 1, :] = one[2:3, :]
-        posbuf[c : c + 1, :] = jnp.where(one[2:3, :] > 0, offset + lane, -1)
-        offset = offset + one[3:4, :]
-
-    lanes = posbuf.shape
-    origin = 2 * lax.broadcasted_iota(jnp.int32, lanes, 0) + (
-        lax.broadcasted_iota(jnp.int32, lanes, 1) >= peers
-    ).astype(jnp.int32)
+        cellbuf[c : c + 1, :] = one[:, 0:width]
+        workbuf[c : c + 1, :] = one[:, width : 2 * width]
+        alive = one[:, width : 2 * width] > 0
+        posbuf[c : c + 1, :] = jnp.where(alive, offset + slot_of, -1)
+        offset = offset + one[:, 2 * width : 3 * width]
+
+    shape = posbuf.shape
+    lanes = lax.broadcasted_iota(jnp.int32, shape, 1)
+    upper = lanes >= slots
+    second = jnp.where(upper, lanes - slots, lanes) >= peers
+    origin = 2 * lax.broadcasted_iota(jnp.int32, shape, 0) + second.astype(jnp.int32)
 
     def place(q, carry):
         hit = posbuf[...] == q * peers + gy
-
-        def picked(values):
-            return jnp.sum(jnp.where(hit, values, 0))
-
-        mrow[q] = picked(rowbuf[...])
-        mcol[q] = picked(colbuf[...])
-        mwork[q] = picked(workbuf[...])
-        source[q] = picked(origin)
+        low, high = hit & ~upper, hit & upper
+
+        def picked(where, values):
+            return jnp.sum(jnp.where(where, values, 0))
+
+        mrow[q] = picked(low, cellbuf[...])
+        mcol[q] = picked(high, cellbuf[...])
+        mwork[q] = picked(low, workbuf[...])
+        source[q] = picked(low, origin)
         return carry
 
     lax.fori_loop(0, slots // 2, place, 0)
 
-    pending = []
-
-    def flush():
-        while pending:
-            hop, slot = pending.pop()
+    def add_y(g, dz):
+        whole_wait(yrecv.at[g], y_rx.at[g, 0])
+        whole_wait(ysrecv.at[g], y_rx.at[g, 1])
+        begin = y * per_y + (z + dz) % nz * vb
+        for v in range(vb):
+            total = partial(begin + v)
+            for dy in range(1, ny):
+                total = total + widened(yrecv[g, dy - 1, v], ysrecv[g, dy - 1, v : v + 1, :])
+            ysum[g % 2, v] = total
+
+    def send_z(dz):
+        for slot, hop, begin, count in z_sends(dz, nz, vb):
+            rows = pl.ds(begin, count)
             send_piece(
-                zq.at[slot],
+                zq.at[slot, rows],
                 zs.at[slot],
-                zrecv.at[slot],
+                zrecv.at[slot, rows],
                 zsrecv.at[slot],
                 z_tx,
                 z_rx.at[slot],
                 y * nz + (z + hop) % nz,
             )
 
-    def arrived(slot):
-        whole_wait(zrecv.at[slot], z_rx.at[slot, 0])
-        whole_wait(zsrecv.at[slot], z_rx.at[slot, 1])
-
+    add_y(0, groups[0])
     for g, dz in enumerate(groups):
-        hop, slot = z_route(dz, nz)
-        whole_wait(yrecv.at[g], y_rx.at[g, 0])
-        whole_wait(ysrecv.at[g], y_rx.at[g, 1])
-        extra = collected(dz, nz)
-        for other in extra:
-            arrived(z_route(other, nz)[1])
-        begin = y * per_y + (z + dz) % nz * vb
+        carried = z_carried(dz, nz, vb)
+        for slot, begin, count in carried:
+            whole_wait(zrecv.at[slot, pl.ds(begin, count)], z_rx.at[slot, 0])
+            whole_wait(zsrecv.at[slot], z_rx.at[slot, 1])
         for v in range(vb):
-            total = partial(begin + v)
-            for dy in range(1, ny):
-                total = total + widened(yrecv[g, dy - 1, v], ysrecv[g, dy - 1, v : v + 1, :])
-            for other in extra:
-                at = z_route(other, nz)[1]
-                total = total + widened(zrecv[at, v], zsrecv[at, v : v + 1, :])
+            total = ysum[g % 2, v]
+            for slot, begin, count in carried:
+                if begin <= v < begin + count:
+                    total = total + widened(zrecv[slot, v], zsrecv[slot, v : v + 1, :])
             if dz == 0:
                 prod[v] = total
             else:
                 coded, scale = narrowed(total)
-                zq[slot, v] = coded
-                zs[slot, v : v + 1, :] = scale
-        flush()
+                for slot, hop, begin, count in z_sends(dz, nz, vb):
+                    if begin <= v < begin + count:
+                        zq[slot, v] = coded
+                        zs[slot, v : v + 1, :] = scale
         if dz:
-            pending.append((hop, slot))
-    flush()
-    for dz in groups:
-        hop, slot = z_route(dz, nz)
-        if dz and hop == dz:
-            arrived(slot)
-            for v in range(vb):
-                prod[v] = prod[v] + widened(zrecv[slot, v], zsrecv[slot, v : v + 1, :])
-
+            add_y(g + 1, groups[g + 1])
+            send_z(dz)
+            more(PER)
+
+    more(99)
     whole_wait(recvbuf.at[pl.ds(0, 2 * (peers - 1))], vals_rx)
 
     def settle(q, carry):
@@ -383,11 +405,12 @@
     lax.fori_loop(0, slots // 2, settle, 0, unroll=4)
 
     whole_wait(metabuf.at[pl.ds(0, peers - 1)], meta_tx)
-    whole_wait(xbuf.at[pl.ds(0, (nx - 1) * vb)], feat_tx)
+    whole_wait(xbuf.at[pl.ds(0, nx // 2 * vb)], feat_tx)
+    whole_wait(xbuf.at[pl.ds(0, (nx // 2 - 1) * vb)], pass_tx)
     whole_wait(recvbuf.at[pl.ds(0, 2 * (peers - 1))], vals_tx)
     whole_wait(yrecv, y_tx.at[0])
     whole_wait(ysrecv, y_tx.at[1])
-    whole_wait(zrecv, z_tx.at[0])
+    whole_wait(zrecv.at[pl.ds(0, nz - 1)], z_tx.at[0])
     whole_wait(zsrecv, z_tx.at[1])
 
 
@@ -431,22 +454,23 @@
             vmem((slots, order, order), bf16),
             vmem((nx * vb, order, width), bf16),
             vmem((slots, order, width), f32),
-            vmem((peers, 8, 128), i32),
-            *[vmem((peers, 128), i32)] * 4,
+            vmem((peers, 1, 6 * slots), i32),
+            *[vmem((peers, 2 * slots), i32)] * 3,
             vmem((nz, ny - 1, vb, order, width), i16),
             vmem((nz, ny - 1, 8, width), f32),
             vmem((nz, ny - 1, vb, order, width), i16),
             vmem((nz, ny - 1, 8, width), f32),
-            vmem((nz - 1, vb, order, width), i16),
-            vmem((nz - 1, 8, width), f32),
-            vmem((nz - 1, vb, order, width), i16),
-            vmem((nz - 1, 8, width), f32),
+            vmem((2, vb, order, width), f32),
+            vmem((nz, vb, order, width), i16),
+            vmem((nz, 8, width), f32),
+            vmem((nz, vb, order, width), i16),
+            vmem((nz, 8, width), f32),
             smem((slots // 2,), i32),
-            pltpu.SemaphoreType.DMA((15,)),
+            pltpu.SemaphoreType.DMA((17,)),
             pltpu.SemaphoreType.DMA((2,)),
             pltpu.SemaphoreType.DMA((nz, 2)),
             pltpu.SemaphoreType.DMA((2,)),
-            pltpu.SemaphoreType.DMA((nz - 1, 2)),
+            pltpu.SemaphoreType.DMA((nz, 2)),
         ],
         compiler_params=pltpu.CompilerParams(
             collective_id=0, has_side_effects=True, vmem_limit_bytes=67043328

time: 77.4 us -> 75.7 us (0.978)
  the two profiles are of different devices: /device:TPU:32 before, /device:TPU:1 now
where the time goes in v4:
time: 75.7 us; the launch traced here: 75.5 us
  Pallas kernels  74.9 us (99%)
    pallas_call x1, Pallas kernels, on_device(): pl.pallas_call(functools.partial(kernel, sizes), out_shape=shapes, in_spe...  72.5 us
    pallas_call x1, Pallas kernels, on_device(): pl.pallas_call(deliver, out_shape=shapes, in_specs=[in_vmem, in_vmem, in_...  2.4 us

profile of v4, /device:TPU:1, one launch (start us, length us, event | category | flops | bytes accessed | tf_op | source)
XLA Modules:
  0.0 75.5 jit_solution(13495785230547610098)
XLA Ops:
  0.6 72.5 %shard_map.92 = (f32[2,128,128]{2,1,0:T(8,128)}, bf16[32,128,128]{2,1,0:T(8,128)(2,1)}, s32[32]{0:T(128)}, s32[32]{0:T(128)}, s32[32]{0:T(128)}) custom-call(bf16[2,128,128]{2,1,0:T(8,128)(2,1)} %bitcast.5, bf16[64,128,128]{2,1,0:T(8,128)(2,1)} %tiles_hbm.1, s32[64]{0:T(128)} %row_hbm.1, s32[64]{0:T(128)} %col_hbm.1, s32[64]{0:T(128)} %work_hbm.1, ...), custom_call_target="tpu_custom_call" | custom-call | tf_op jit(solution)/shard_map/pallas_call | solution.py:442
  73.1 2.4 %shard_map.93 = (f32[2,128,128]{2,1,0:T(8,128)}, bf16[32,128,128]{2,1,0:T(8,128)(2,1)}, s32[32]{0:T(128)}, s32[32]{0:T(128)}, s32[32]{0:T(128)}) custom-call(f32[2,128,128]{2,1,0:T(8,128)} %get-tuple-element.15.refs_0_, bf16[32,128,128]{2,1,0:T(8,128)(2,1)} %get-tuple-element.16.refs_1_, s32[32]{0:T(128)} %get-tuple-element.17.refs_2_, ...), custom_call_target="tpu_custom_call" | custom-call | tf_op jit(solution)/shard_map/pallas_call | solution.py:488

commit v5 on v4

--- a/solution.py
+++ b/solution.py
@@ -8,9 +8,9 @@
 from jax.sharding import PartitionSpec as P
 
 NZ = 8
-UP = 16
-AFTERY = 8
-PER = 1
+UP = 14
+AFTERY = 7
+PER = 2
 LIMIT = 32000.0
 TINY = 1e-30
 MESH = pl.DeviceIdType.MESH
@@ -74,6 +74,11 @@
     row_line,
     col_line,
     work_line,
+    prod_hbm,
+    moved_hbm,
+    mrow_hbm,
+    mcol_hbm,
+    mwork_hbm,
     prod,
     moved,
     mrow,
@@ -347,6 +352,12 @@
         return carry
 
     lax.fori_loop(0, slots // 2, place, 0)
+    leaving = [
+        pltpu.make_async_copy(src, dst, sems.at[17 + i])
+        for i, (src, dst) in enumerate(((mrow, mrow_hbm), (mcol, mcol_hbm), (mwork, mwork_hbm)))
+    ]
+    for copy in leaving:
+        copy.start()
 
     def add_y(g, dz):
         whole_wait(yrecv.at[g], y_rx.at[g, 0])
@@ -395,6 +406,8 @@
             send_z(dz)
             more(PER)
 
+    leaving.append(pltpu.make_async_copy(prod, prod_hbm, sems.at[20]))
+    leaving[-1].start()
     more(99)
     whole_wait(recvbuf.at[pl.ds(0, 2 * (peers - 1))], vals_rx)
 
@@ -402,7 +415,12 @@
         moved[q] = recvbuf[source[q]]
         return carry
 
-    lax.fori_loop(0, slots // 2, settle, 0, unroll=4)
+    batch = slots // 8
+    for i in range(4):
+        lax.fori_loop(i * batch, (i + 1) * batch, settle, 0, unroll=2)
+        rows = pl.ds(i * batch, batch)
+        leaving.append(pltpu.make_async_copy(moved.at[rows], moved_hbm.at[rows], sems.at[21 + i]))
+        leaving[-1].start()
 
     whole_wait(metabuf.at[pl.ds(0, peers - 1)], meta_tx)
     whole_wait(xbuf.at[pl.ds(0, nx // 2 * vb)], feat_tx)
@@ -412,16 +430,25 @@
     whole_wait(ysrecv, y_tx.at[1])
     whole_wait(zrecv.at[pl.ds(0, nz - 1)], z_tx.at[0])
     whole_wait(zsrecv, z_tx.at[1])
+    for copy in leaving:
+        copy.wait()
 
 
 def deliver(*refs):
-    count = len(refs) // 2
-    outs, sems = refs[count : 2 * count], refs[-1]
-    copies = [pltpu.make_async_copy(refs[i], outs[i], sems.at[i]) for i in range(count)]
-    for copy in copies:
-        copy.start()
-    for copy in copies:
-        copy.wait()
+    ins, outs, held, in_sems, out_sems = refs[:5], refs[5:10], refs[10:15], refs[15], refs[16]
+    batch = ins[1].shape[0] // 4
+    steps = [(i, slice(None)) for i in (0, 2, 3, 4)]
+    steps = [(1, pl.ds(g * batch, batch)) for g in range(4)] + steps
+    arriving, leaving = [], []
+    for n, (i, rows) in enumerate(steps):
+        arriving.append(pltpu.make_async_copy(ins[i].at[rows], held[i].at[rows], in_sems.at[n]))
+        leaving.append(pltpu.make_async_copy(held[i].at[rows], outs[i].at[rows], out_sems.at[n]))
+        arriving[-1].start()
+    for arrive, leave in zip(arriving, leaving, strict=True):
+        arrive.wait()
+        leave.start()
+    for leave in leaving:
+        leave.wait()
 
 
 def on_device(sizes, features, tile_vals, tile_row, tile_col, tile_work):
@@ -433,7 +460,12 @@
     per_y = nz * vb
     bf16, f32, i32, i16 = jnp.bfloat16, jnp.float32, jnp.int32, jnp.int16
     vmem, smem = pltpu.VMEM, pltpu.SMEM
-    in_vmem, in_smem = pl.BlockSpec(memory_space=vmem), pl.BlockSpec(memory_space=smem)
+    in_hbm = pl.BlockSpec(memory_space=pltpu.HBM)
+    results_held = [
+        vmem((vb, order, width), f32),
+        vmem((slots // 2, order, order), bf16),
+        *[smem((slots // 2,), i32)] * 3,
+    ]
     shapes = (
         jax.ShapeDtypeStruct((vb, order, width), f32),
         jax.ShapeDtypeStruct((slots // 2, order, order), bf16),
@@ -442,9 +474,10 @@
     results = pl.pallas_call(
         functools.partial(kernel, sizes),
         out_shape=shapes,
-        in_specs=[pl.BlockSpec(memory_space=pltpu.HBM)] * 8,
-        out_specs=(in_vmem, in_vmem, in_smem, in_smem, in_smem),
+        in_specs=[in_hbm] * 8,
+        out_specs=[in_hbm] * 5,
         scratch_shapes=[
+            *results_held,
             *[smem((slots,), i32)] * 3,
             smem((1, slots + peers * vb), i32),
             *[vmem((1, slots), i32)] * 3,
@@ -466,7 +499,7 @@
             vmem((nz, vb, order, width), i16),
             vmem((nz, 8, width), f32),
             smem((slots // 2,), i32),
-            pltpu.SemaphoreType.DMA((17,)),
+            pltpu.SemaphoreType.DMA((25,)),
             pltpu.SemaphoreType.DMA((2,)),
             pltpu.SemaphoreType.DMA((nz, 2)),
             pltpu.SemaphoreType.DMA((2,)),
@@ -488,9 +521,9 @@
     prod, moved, mrow, mcol, mwork = pl.pallas_call(
         deliver,
         out_shape=shapes,
-        in_specs=[in_vmem, in_vmem, in_smem, in_smem, in_smem],
-        out_specs=[pl.BlockSpec(memory_space=pltpu.HBM)] * 5,
-        scratch_shapes=[pltpu.SemaphoreType.DMA((5,))],
+        in_specs=[in_hbm] * 5,
+        out_specs=[in_hbm] * 5,
+        scratch_shapes=[*results_held, *[pltpu.SemaphoreType.DMA((8,))] * 2],
     )(*results)
     return prod.reshape(vb * order, width), moved, mrow, mcol, mwork
 

time: 75.7 us -> 74 us (0.978)
  the two profiles are of different devices: /device:TPU:1 before, /device:TPU:32 now
where the time goes in v5:
time: 74 us; the launch traced here: 72.6 us
  Pallas kernels  71.9 us (97%)
    pallas_call x1, Pallas kernels, on_device(): pl.pallas_call(functools.partial(kernel, sizes), out_shape=shapes, in_spe...  69.8 us
    pallas_call x1, Pallas kernels, on_device(): pl.pallas_call(deliver, out_shape=shapes, in_specs=[in_hbm] * 5, out_spec...  2.12 us

profile of v5, /device:TPU:32, one launch (start us, length us, event | category | flops | bytes accessed | tf_op | source)
XLA Modules:
  0.0 72.6 jit_solution(1808232132540777523)
XLA Ops:
  0.6 69.8 %shard_map.92 = (f32[2,128,128]{2,1,0:T(8,128)}, bf16[32,128,128]{2,1,0:T(8,128)(2,1)}, s32[32]{0:T(128)}, s32[32]{0:T(128)}, s32[32]{0:T(128)}) custom-call(bf16[2,128,128]{2,1,0:T(8,128)(2,1)} %bitcast.5, bf16[64,128,128]{2,1,0:T(8,128)(2,1)} %tiles_hbm.1, s32[64]{0:T(128)} %row_hbm.1, s32[64]{0:T(128)} %col_hbm.1, s32[64]{0:T(128)} %work_hbm.1, ...), custom_call_target="tpu_custom_call" | custom-call | tf_op jit(solution)/shard_map/pallas_call | solution.py:474
  70.5 2.1 %shard_map.93 = (f32[2,128,128]{2,1,0:T(8,128)}, bf16[32,128,128]{2,1,0:T(8,128)(2,1)}, s32[32]{0:T(128)}, s32[32]{0:T(128)}, s32[32]{0:T(128)}) custom-call(f32[2,128,128]{2,1,0:T(8,128)} %get-tuple-element.15.refs_0_, bf16[32,128,128]{2,1,0:T(8,128)(2,1)} %get-tuple-element.16.refs_1_, s32[32]{0:T(128)} %get-tuple-element.17.refs_2_, ...), custom_call_target="tpu_custom_call" | custom-call | tf_op jit(solution)/shard_map/pallas_call | solution.py:521

commit v6 on v5

--- a/solution.py
+++ b/solution.py
@@ -274,7 +274,7 @@
         sums[t] = product + jnp.where(prev >= 0, sums[jnp.maximum(prev, 0)], 0.0)
         return carry
 
-    lax.fori_loop(0, slots, multiply, 0, unroll=4)
+    lax.fori_loop(0, slots, multiply, 0, unroll=8)
 
     def partial(r):
         last = chain_s[0, slots + r]
@@ -315,7 +315,7 @@
             ys[g, dy - 1, pl.ds(v, 1), :] = scale
             return carry
 
-        lax.fori_loop(0, (ny - 1) * vb, code_y, 0, unroll=2)
+        lax.fori_loop(0, (ny - 1) * vb, code_y, 0, unroll=6)
         if g:
             send_y(g - 1)
     send_y(len(groups) - 1)

time: 74 us -> 73.5 us (level)
  no operation moved by 1% of the time
where the time goes in v6:
time: 73.5 us; the launch traced here: 72.3 us
  Pallas kernels  71.7 us (98%)
    pallas_call x1, Pallas kernels, on_device(): pl.pallas_call(functools.partial(kernel, sizes), out_shape=shapes, in_spe...  69.5 us
    pallas_call x1, Pallas kernels, on_device(): pl.pallas_call(deliver, out_shape=shapes, in_specs=[in_hbm] * 5, out_spec...  2.12 us

profile of v6, /device:TPU:32, one launch (start us, length us, event | category | flops | bytes accessed | tf_op | source)
XLA Modules:
  0.0 72.3 jit_solution(16034211249218309120)
XLA Ops:
  0.6 69.5 %shard_map.92 = (f32[2,128,128]{2,1,0:T(8,128)}, bf16[32,128,128]{2,1,0:T(8,128)(2,1)}, s32[32]{0:T(128)}, s32[32]{0:T(128)}, s32[32]{0:T(128)}) custom-call(bf16[2,128,128]{2,1,0:T(8,128)(2,1)} %bitcast.5, bf16[64,128,128]{2,1,0:T(8,128)(2,1)} %tiles_hbm.1, s32[64]{0:T(128)} %row_hbm.1, s32[64]{0:T(128)} %col_hbm.1, s32[64]{0:T(128)} %work_hbm.1, ...), custom_call_target="tpu_custom_call" | custom-call | tf_op jit(solution)/shard_map/pallas_call | solution.py:474
  70.2 2.1 %shard_map.93 = (f32[2,128,128]{2,1,0:T(8,128)}, bf16[32,128,128]{2,1,0:T(8,128)(2,1)}, s32[32]{0:T(128)}, s32[32]{0:T(128)}, s32[32]{0:T(128)}) custom-call(f32[2,128,128]{2,1,0:T(8,128)} %get-tuple-element.15.refs_0_, bf16[32,128,128]{2,1,0:T(8,128)(2,1)} %get-tuple-element.16.refs_1_, s32[32]{0:T(128)} %get-tuple-element.17.refs_2_, ...), custom_call_target="tpu_custom_call" | custom-call | tf_op jit(solution)/shard_map/pallas_call | solution.py:521
